TPU v7x, 16 devices: a whole 2x2x2 slice. The times are simulated.
16 devices in a mesh: rep: 1, dp: 16 (over x, y, z, core).
Axes of the slice: x: 2, y: 2, z: 2, core: 2. Of those that a mesh axis runs over, the one named last changes fastest.
Arguments:
- x: bfloat16 [16, 2048, 1024], P(('rep', 'dp'))
- dy: bfloat16 [16, 2048, 1024], P(('rep', 'dp'))
- w_gate: bfloat16 [2, 1024, 3200], P(None, 'dp')
- w_up: bfloat16 [2, 1024, 3200], P(None, 'dp')
- w_down: bfloat16 [2, 3200, 1024], P(None, 'dp')
- m_w_gate: float32 [2, 1024, 3200], P(None, 'dp')
- m_w_up: float32 [2, 1024, 3200], P(None, 'dp')
- m_w_down: float32 [2, 3200, 1024], P(None, 'dp')
- v_w_gate: float32 [2, 1024, 3200], P(None, 'dp')
- v_w_up: float32 [2, 1024, 3200], P(None, 'dp')
- v_w_down: float32 [2, 3200, 1024], P(None, 'dp')
Outputs:
- output 1: bfloat16 [2, 1024, 3200], P('rep', 'dp')
- output 2: bfloat16 [2, 1024, 3200], P('rep', 'dp')
- output 3: bfloat16 [2, 3200, 1024], P('rep', 'dp')
- output 4: float32 [2, 1024, 3200], P('rep', 'dp')
- output 5: float32 [2, 1024, 3200], P('rep', 'dp')
- output 6: float32 [2, 3200, 1024], P('rep', 'dp')
- output 7: float32 [2, 1024, 3200], P('rep', 'dp')
- output 8: float32 [2, 1024, 3200], P('rep', 'dp')
- output 9: float32 [2, 3200, 1024], P('rep', 'dp')
All inputs are finite; a program needn't handle non-finite values.
Results may differ from a plain program's by a relative error of at most 0.0223.
Values are sent between devices in bfloat16 or wider.
A program may use at most 2 GiB of HBM per device.

v0:
```python
import jax
import jax.numpy as jnp
from jax import lax
from jax.sharding import PartitionSpec as P

NAMES = ("w_gate", "w_up", "w_down")


def matmul(a, w):
    return jnp.dot(a, w, preferred_element_type=jnp.float32).astype(jnp.bfloat16)


def normed(h):
    wide = h.astype(jnp.float32)
    scale = lax.rsqrt(jnp.mean(wide**2, -1, keepdims=True) + 1e-6)
    return (wide * scale).astype(jnp.bfloat16)


def layer(h, w):
    a = normed(h)
    gate = jnp.dot(a, w["w_gate"], preferred_element_type=jnp.float32)
    up = jnp.dot(a, w["w_up"], preferred_element_type=jnp.float32)
    return h + matmul((jax.nn.silu(gate) * up).astype(jnp.bfloat16), w["w_down"])


def adamw(w, m, v, g):
    m = 0.9 * m + 0.1 * g
    v = 0.95 * v + 0.05 * g * g
    step = m * lax.rsqrt(v + 1e-8) + 0.1 * w
    return (w - 0.02 * step).astype(jnp.bfloat16), m, v


def clipped(gradients, sum_of_squares, count):
    factor = jnp.minimum(1.0, 0.5 * lax.rsqrt(sum_of_squares / count + 1e-30))
    return [g * factor for g in gradients]


def solution(mesh):
    def fetched(weights, number):
        return {name: lax.all_gather(w[number], "dp", axis=0, tiled=True) for name, w in zip(NAMES, weights, strict=True)}

    def step(x, dy, *arrays):
        weights, m, v = (arrays[i : i + 3] for i in (0, 3, 6))
        layers = weights[0].shape[0]
        h, kept = x[0], []
        for number in range(layers):
            kept.append(h)
            h = layer(h, fetched(weights, number))
        by_h, mine = dy[0], [None] * layers
        for number in reversed(range(layers)):
            _, back = jax.vjp(lambda w, h: layer(h, w), fetched(weights, number), kept[number])
            by_w, by_h = back(by_h)
            mine[number] = [lax.psum_scatter(by_w[name], "dp", scatter_dimension=0, tiled=True) for name in NAMES]
        gradients = [jnp.stack([mine[number][i] for number in range(layers)]).astype(jnp.float32) for i in range(3)]
        squares = lax.psum(sum(jnp.sum(g * g) for g in gradients), "dp")
        gradients = clipped(gradients, squares, lax.psum(1, "dp") * sum(g.size for g in gradients))
        new = [adamw(w.astype(jnp.float32), m, v, g) for w, m, v, g in zip(weights, m, v, gradients, strict=True)]
        return tuple(one[which] for which in range(3) for one in new)

    states, cut = P(("rep", "dp"), None, None), P(None, "dp", None)
    return jax.shard_map(
        step,
        mesh=mesh,
        in_specs=(states, states) + (cut,) * 9,
        out_specs=(P("rep", "dp", None),) * 9,
        check_vma=False,
    )
```

profile of v0, /device:TPU:0, one launch (start us, length us, event | category | flops | bytes accessed | tf_op | source)
XLA Modules:
  0.0 917.3 jit_solution(14670829899451229301)
XLA Ops:
  15.4 6.5 copy.20
  21.9 3.1 fusion.15
  25.0 6.6 copy.21
  31.5 24.8 %all-gather.13.cloned.1.call-done = bf16[1,1024,3200]{2,1,0:T(8,128)(2,1)} async-done(((bf16[1,64,3200]{2,1,0:T(8,128)(2,1)}), bf16[1,1024,3200]{2,1,0:T(8,128)(2,1)}) %all-gather.13.cloned.1.call-update) | async-done | bytes 6553616 | tf_op jit(solution)/shard_map/all_gather | solution.py:40
  56.4 22.9 %fusion.41 = f32[2048,3200]{1,0:T(8,128)} fusion(bf16[1,1024,3200]{2,1,0:T(8,128)(2,1)} %all-gather.13.cloned.1.call-done, bf16[1,2048,1024]{1,2,0:T(8,128)(2,1)} %copy.20, f32[2048]{0:T(1024)S(1)} %add_rsqrt_fusion), kind=kOutput, calls=%fused_computation.59 | convolution fusion | flops 13428064256 | bytes 36970496 | tf_op jit(solution)/shard_map/dot_general | solution.py:21
  79.3 22.6 %all-gather.15.cloned.1.call-done = bf16[1,1024,3200]{2,1,0:T(8,128)(2,1)} async-done(((bf16[1,64,3200]{2,1,0:T(8,128)(2,1)}), bf16[1,1024,3200]{2,1,0:T(8,128)(2,1)}) %all-gather.15.cloned.1.call-update) | async-done | bytes 6553616 | tf_op jit(solution)/shard_map/all_gather | solution.py:40
  101.9 31.4 %multiply_convert_fusion.1 = (bf16[2048,3200]{1,0:T(8,128)(2,1)}, f32[2048,3200]{1,0:T(8,128)}) fusion(f32[2048,3200]{1,0:T(8,128)} %fusion.41, bf16[1,1024,3200]{2,1,0:T(8,128)(2,1)} %all-gather.15.cloned.1.call-done, bf16[1,2048,1024]{1,2,0:T(8,128)(2,1)} %copy.20, f32[2048]{0:T(1024)S(1)} %add_rsqrt_fusion), kind=kOutput, calls=%fused_computation.17 | convolution fusion | flops 13467385856 | bytes 76292096 | tf_op jit(solution)/shard_map/dot_general | solution.py:22
  133.3 14.2 %all-gather.17.cloned.1.call-done = bf16[1,3200,1024]{2,1,0:T(8,128)(2,1)} async-done(((bf16[1,200,1024]{2,1,0:T(8,128)(2,1)}), bf16[1,3200,1024]{2,1,0:T(8,128)(2,1)}) %all-gather.17.cloned.1.call-update) | async-done | bytes 6553616 | tf_op jit(solution)/shard_map/all_gather | solution.py:40
  147.4 21.8 %fusion.19 = (f32[2048]{0:T(1024)S(1)}, bf16[2048,1024]{0,1:T(8,128)(2,1)}) fusion(bf16[2048,3200]{1,0:T(8,128)(2,1)} %get-tuple-element.24, bf16[1,3200,1024]{2,1,0:T(8,128)(2,1)} %all-gather.17.cloned.1.call-done, bf16[1,2048,1024]{1,2,0:T(8,128)(2,1)} %copy.20), kind=kOutput, calls=%fused_computation.37 | convolution fusion | flops 13432256512 | bytes 28057600 | tf_op jit(solution)/shard_map/dot_general | solution.py:10
  169.3 23.5 %all-gather.21.cloned.1.call-done = bf16[1,3200,1024]{2,1,0:T(8,128)(2,1)} async-done(((bf16[1,200,1024]{2,1,0:T(8,128)(2,1)}), bf16[1,3200,1024]{2,1,0:T(8,128)(2,1)}) %all-gather.21.cloned.1.call-update) | async-done | bytes 6553616 | tf_op jit(solution)/shard_map/all_gather | solution.py:40
  192.8 20.9 %convolution_convert_fusion.1 = bf16[2048,3200]{1,0:T(8,128)(2,1)} fusion(bf16[1,3200,1024]{2,1,0:T(8,128)(2,1)} %all-gather.21.cloned.1.call-done, bf16[1,2048,1024]{2,1,0:T(8,128)(2,1)} %param.12), kind=kOutput, calls=%fused_computation.23 | convolution fusion | flops 13428326400 | bytes 23855104 | tf_op jit(solution)/shard_map/transpose(jvp())/dot_general | solution.py:10
  213.8 24.4 %all-gather.23.cloned.1.call-done = bf16[1,1024,3200]{2,1,0:T(8,128)(2,1)} async-done(((bf16[1,64,3200]{2,1,0:T(8,128)(2,1)}), bf16[1,1024,3200]{2,1,0:T(8,128)(2,1)}) %all-gather.23.cloned.1.call-update) | async-done | bytes 6553616 | tf_op jit(solution)/shard_map/all_gather | solution.py:40
  238.2 22.8 %fusion.28 = f32[2048,3200]{1,0:T(8,128)} fusion(bf16[1,1024,3200]{2,1,0:T(8,128)(2,1)} %all-gather.23.cloned.1.call-done, bf16[2048,1024]{0,1:T(8,128)(2,1)} %get-tuple-element.27, f32[2048]{0:T(1024)S(1)} %fusion.80), kind=kOutput, calls=%fused_computation.46 | convolution fusion | flops 13428064256 | bytes 36970496 | tf_op jit(solution)/shard_map/jvp()/dot_general | solution.py:22
  261.0 22.6 %all-gather.19.cloned.1.call-done = bf16[1,1024,3200]{2,1,0:T(8,128)(2,1)} async-done(((bf16[1,64,3200]{2,1,0:T(8,128)(2,1)}), bf16[1,1024,3200]{2,1,0:T(8,128)(2,1)}) %all-gather.19.cloned.1.call-update) | async-done | bytes 6553616 | tf_op jit(solution)/shard_map/all_gather | solution.py:40
  283.6 38.7 %fusion.2 = (bf16[2048,3200]{1,0:T(8,128)(2,1)}, f32[2048,3200]{1,0:T(8,128)}) fusion(f32[2048,3200]{1,0:T(8,128)} %fusion.28, bf16[2048,3200]{1,0:T(8,128)(2,1)} %convolution_convert_fusion.1, bf16[1,1024,3200]{2,1,0:T(8,128)(2,1)} %all-gather.19.cloned.1.call-done, bf16[2048,1024]{0,1:T(8,128)(2,1)} %get-tuple-element.27, f32[2048]{0:T(1024)S(1)} %fusion.80), kind=kOutput, calls=%fused_computation.8 | convolution fusion | flops 13506707456 | bytes 89399296 | tf_op jit(solution)/shard_map/jvp()/dot_general | solution.py:21
  322.4 22.6 %fusion.12 = bf16[2048,1024]{0,1:T(8,128)(2,1)} fusion(bf16[2048,3200]{1,0:T(8,128)(2,1)} %convolution_convert_fusion.1, bf16[1,1024,3200]{2,1,0:T(8,128)(2,1)} %all-gather.23.cloned.1.call-done, f32[2048,3200]{1,0:T(8,128)} %get-tuple-element.29), kind=kOutput, calls=%fused_computation.21 | convolution fusion | flops 13461094400 | bytes 50069504 | tf_op jit(solution)/shard_map/transpose(jvp())/dot_general | solution.py:22
  344.9 21.8 %fusion.21 = (f32[2048]{0:T(1024)S(1)}, bf16[2048,1024]{0,1:T(8,128)(2,1)}) fusion(bf16[2048,1024]{0,1:T(8,128)(2,1)S(1)} %copy-done.2, bf16[2048,1024]{0,1:T(8,128)(2,1)} %fusion.12, bf16[2048,3200]{1,0:T(8,128)(2,1)} %get-tuple-element.28, bf16[1,1024,3200]{2,1,0:T(8,128)(2,1)} %all-gather.19.cloned.1.call-done), kind=kOutput, calls=%fused_computation.39 | convolution fusion | flops 13432256512 | bytes 32251904 | tf_op jit(solution)/shard_map/transpose(jvp())/dot_general | solution.py:21
  366.8 4.9 fusion.44
  373.7 19.5 %convolution_convert_fusion.2 = bf16[3200,1024]{1,0:T(8,128)(2,1)} fusion(bf16[2048,3200]{1,0:T(8,128)(2,1)} %get-tuple-element.24, bf16[2048,1024]{0,1:T(8,128)(2,1)S(1)} %fusion.44), kind=kOutput, calls=%fused_computation.44 | convolution fusion | flops 13425049600 | bytes 23855104 | tf_op jit(solution)/shard_map/transpose(jvp())/dot_general | solution.py:10
  393.3 26.1 %fusion.25 = bf16[3200,1024]{1,0:T(8,128)(2,1)} fusion(f32[2048,3200]{1,0:T(8,128)} %fusion.28, bf16[1,2048,1024]{2,1,0:T(8,128)(2,1)} %param.12, f32[2048,3200]{1,0:T(8,128)} %get-tuple-element.29), kind=kOutput, calls=%fused_computation.41 | convolution fusion | flops 13464371200 | bytes 63176704 | tf_op jit(solution)/shard_map/transpose(jvp())/dot_general | solution.py:10
  419.5 21.4 %convolution_convert_fusion = bf16[2048,3200]{1,0:T(8,128)(2,1)} fusion(bf16[2048,1024]{0,1:T(8,128)(2,1)} %copy-done.3, bf16[1,3200,1024]{2,1,0:T(8,128)(2,1)} %all-gather.17.cloned.1.call-done), kind=kOutput, calls=%fused_computation.22 | convolution fusion | flops 13428326400 | bytes 23855104 | tf_op jit(solution)/shard_map/transpose(jvp())/dot_general | solution.py:10
  440.9 24.2 %fusion.27 = bf16[1024,3200]{1,0:T(8,128)(2,1)} fusion(bf16[2048,3200]{1,0:T(8,128)(2,1)} %convolution_convert_fusion, f32[2048,3200]{1,0:T(8,128)} %fusion.41, bf16[1,2048,1024]{1,2,0:T(8,128)(2,1)S(1)} %copy-done.1, f32[2048]{0:T(1024)S(1)} %copy-done.20), kind=kOutput, calls=%fused_computation.43 | convolution fusion | flops 13470662656 | bytes 50077696 | tf_op jit(solution)/shard_map/transpose(jvp())/dot_general | solution.py:22
  465.8 25.2 %fusion.26 = bf16[1024,3200]{1,0:T(8,128)(2,1)} fusion(bf16[2048,3200]{1,0:T(8,128)(2,1)} %convolution_convert_fusion.1, bf16[2048,1024]{0,1:T(8,128)(2,1)} %get-tuple-element.27, f32[2048]{0:T(1024)S(1)} %copy-done.16, f32[2048,3200]{1,0:T(8,128)} %get-tuple-element.29), kind=kOutput, calls=%fused_computation.42 | convolution fusion | flops 13470662656 | bytes 50077696 | tf_op jit(solution)/shard_map/transpose(jvp())/dot_general | solution.py:22
  491.2 32.7 %fusion.22 = bf16[1024,3200]{1,0:T(8,128)(2,1)} fusion(f32[2048,3200]{1,0:T(8,128)} %fusion.41, f32[2048,3200]{1,0:T(8,128)} %get-tuple-element.25, bf16[2048,3200]{1,0:T(8,128)(2,1)} %convolution_convert_fusion, bf16[1,2048,1024]{1,2,0:T(8,128)(2,1)} %copy.20, f32[2048]{0:T(1024)S(1)} %copy-done.20), kind=kOutput, calls=%fused_computation.40 | convolution fusion | flops 13503430656 | bytes 76292096 | tf_op jit(solution)/shard_map/transpose(jvp())/dot_general | solution.py:21
  523.9 21.1 %convolution_convert_fusion.3 = bf16[1024,3200]{1,0:T(8,128)(2,1)} fusion(bf16[2048,3200]{1,0:T(8,128)(2,1)} %get-tuple-element.28, bf16[2048,1024]{0,1:T(8,128)(2,1)} %get-tuple-element.27, f32[2048]{0:T(1024)S(1)} %copy-done.16), kind=kOutput, calls=%fused_computation.45 | convolution fusion | flops 13428064256 | bytes 23863296 | tf_op jit(solution)/shard_map/transpose(jvp())/dot_general | solution.py:21
  548.5 76.3 %reduce-scatter.11.cloned.1.call-done = bf16[64,3200]{1,0:T(8,128)(2,1)} async-done(((bf16[1024,3200]{1,0:T(8,128)(2,1)}), bf16[64,3200]{1,0:T(8,128)(2,1)}) %reduce-scatter.11.cloned.1.call-update) | async-done | bytes 409616 | tf_op jit(solution)/shard_map/reduce_scatter | solution.py:53
  624.9 80.1 %reduce-scatter.13.cloned.1.call-done = bf16[64,3200]{1,0:T(8,128)(2,1)} async-done(((bf16[1024,3200]{1,0:T(8,128)(2,1)}), bf16[64,3200]{1,0:T(8,128)(2,1)}) %reduce-scatter.13.cloned.1.call-update) | async-done | bytes 409616 | tf_op jit(solution)/shard_map/reduce_scatter | solution.py:53
  707.1 75.2 %reduce-scatter.7.cloned.1.call-done = bf16[64,3200]{1,0:T(8,128)(2,1)} async-done(((bf16[1024,3200]{1,0:T(8,128)(2,1)}), bf16[64,3200]{1,0:T(8,128)(2,1)}) %reduce-scatter.7.cloned.1.call-update) | async-done | bytes 409616 | tf_op jit(solution)/shard_map/reduce_scatter | solution.py:53
  782.3 79.3 %reduce-scatter.9.cloned.1.call-done = bf16[64,3200]{1,0:T(8,128)(2,1)} async-done(((bf16[1024,3200]{1,0:T(8,128)(2,1)}), bf16[64,3200]{1,0:T(8,128)(2,1)}) %reduce-scatter.9.cloned.1.call-update) | async-done | bytes 409616 | tf_op jit(solution)/shard_map/reduce_scatter | solution.py:53
  865.7 33.9 %psum.7 = f32[]{:T(128)} all-reduce(f32[]{:T(128)S(6)} %add.99), channel_id=1, replica_groups=mesh['rep'=1,'dp'=16] {'dp'}, use_global_device_ids=true, to_apply=%region_12.13 | all-reduce | flops 1 | bytes 8 | tf_op jit(solution)/shard_map/psum | solution.py:55
  900.4 4.9 fusion.76
  906.1 4.2 fusion.67
  (77 shorter events, 19.8 us)
Async XLA Ops:
  7.2 49.2 %all-gather.13.cloned.1.call-start = ((), (), s32[]{:S(2)}) async-start(), calls=%async_computation.12 | async-start | bytes 6963200 | tf_op jit(solution)/shard_map/all_gather | solution.py:40
  9.3 92.6 %all-gather.15.cloned.1.call-start = ((), (), s32[]{:S(2)}) async-start(), calls=%async_computation.13 | async-start | bytes 6963200 | tf_op jit(solution)/shard_map/all_gather | solution.py:40
  11.5 136.0 %all-gather.17.cloned.1.call-start = ((), (), s32[]{:S(2)}) async-start(), calls=%async_computation.14 | async-start | bytes 6963200 | tf_op jit(solution)/shard_map/all_gather | solution.py:40
  13.6 179.2 %all-gather.21.cloned.1.call-start = ((), (), s32[]{:S(2)}) async-start(), calls=%async_computation.16 | async-start | bytes 6963200 | tf_op jit(solution)/shard_map/all_gather | solution.py:40
  14.2 224.0 %all-gather.23.cloned.1.call-start = ((), (), s32[]{:S(2)}) async-start(), calls=%async_computation.17 | async-start | bytes 6963200 | tf_op jit(solution)/shard_map/all_gather | solution.py:40
  14.8 268.9 %all-gather.19.cloned.1.call-start = ((), (), s32[]{:S(2)}) async-start(), calls=%async_computation.15 | async-start | bytes 6963200 | tf_op jit(solution)/shard_map/all_gather | solution.py:40
  15.3 529.7 %reduce-scatter.15.cloned.1.call-start = ((), (), s32[]{:S(2)}) async-start(), calls=%async_computation.10 | async-start | bytes 6963200 | tf_op jit(solution)/shard_map/reduce_scatter | solution.py:53
  25.0 76.9 %copy-start.19 = (f32[2048]{0:T(1024)}, f32[2048]{0:T(1024)S(1)}, u32[]{:S(2)}) copy-start(f32[2048]{0:T(1024)S(1)} %add_rsqrt_fusion) | copy-start | bytes 24580
  169.3 44.5 %copy-start.17 = (f32[2048]{0:T(1024)}, f32[2048]{0:T(1024)S(1)}, u32[]{:S(2)}) copy-start(f32[2048]{0:T(1024)S(1)} %get-tuple-element.26) | copy-start | bytes 24580
  169.3 197.5 %copy-start.15 = (f32[2048]{0:T(1024)}, f32[2048]{0:T(1024)S(1)}, u32[]{:S(2)}) copy-start(f32[2048]{0:T(1024)S(1)} %fusion.80) | copy-start | bytes 24580
  322.3 22.6 %copy-start.2 = (bf16[2048,1024]{0,1:T(8,128)(2,1)S(1)}, bf16[2048,1024]{0,1:T(8,128)(2,1)}, u32[]{:S(2)}) copy-start(bf16[2048,1024]{0,1:T(8,128)(2,1)} %get-tuple-element.27) | copy-start | bytes 12582916
  344.9 21.8 %copy-start.18 = (f32[2048]{0:T(1024)S(1)}, f32[2048]{0:T(1024)}, u32[]{:S(2)}) copy-start(f32[2048]{0:T(1024)} %copy-done.17) | copy-start | bytes 24580
  344.9 21.9 %copy-start = (bf16[1,2048,1024]{1,2,0:T(8,128)(2,1)S(1)}, bf16[1,2048,1024]{1,2,0:T(8,128)(2,1)}, u32[]{:S(2)}) copy-start(bf16[1,2048,1024]{1,2,0:T(8,128)(2,1)} %copy.21) | copy-start | bytes 12582916
  371.7 2.1 copy-start.3
  393.2 153.2 %reduce-scatter.17.cloned.1.call-start = ((), (), s32[]{:S(2)}) async-start(), calls=%async_computation.11 | async-start | bytes 6963200 | tf_op jit(solution)/shard_map/reduce_scatter | solution.py:53
  419.4 21.5 %copy-start.20 = (f32[2048]{0:T(1024)S(1)}, f32[2048]{0:T(1024)}, u32[]{:S(2)}) copy-start(f32[2048]{0:T(1024)} %copy-done.19) | copy-start | bytes 24580
  419.4 205.5 %reduce-scatter.11.cloned.1.call-start = ((), (), s32[]{:S(2)}) async-start(), calls=%async_computation.8 | async-start | bytes 6963200 | tf_op jit(solution)/shard_map/reduce_scatter | solution.py:53
  419.4 21.5 %copy-start.1 = (bf16[1,2048,1024]{1,2,0:T(8,128)(2,1)S(1)}, bf16[1,2048,1024]{1,2,0:T(8,128)(2,1)}, u32[]{:S(2)}) copy-start(bf16[1,2048,1024]{1,2,0:T(8,128)(2,1)} %copy.20) | copy-start | bytes 12582916
  465.2 239.8 %reduce-scatter.13.cloned.1.call-start = ((), (), s32[]{:S(2)}) async-start(), calls=%async_computation.9 | async-start | bytes 6963200 | tf_op jit(solution)/shard_map/reduce_scatter | solution.py:53
  491.1 291.2 %reduce-scatter.7.cloned.1.call-start = ((), (), s32[]{:S(2)}) async-start(), calls=%async_computation.6 | async-start | bytes 6963200 | tf_op jit(solution)/shard_map/reduce_scatter | solution.py:53
  523.8 337.8 %reduce-scatter.9.cloned.1.call-start = ((), (), s32[]{:S(2)}) async-start(), calls=%async_computation.7 | async-start | bytes 6963200 | tf_op jit(solution)/shard_map/reduce_scatter | solution.py:53
  545.0 355.4 %copy-start.4 = (bf16[2,200,1024]{2,1,0:T(8,128)(2,1)S(1)}, bf16[2,200,1024]{2,1,0:T(8,128)(2,1)}, u32[]{:S(2)}) copy-start(bf16[2,200,1024]{2,1,0:T(8,128)(2,1)} %param.15) | copy-start | bytes 2457604
  545.0 360.3 %copy-start.5 = (bf16[2,64,3200]{2,1,0:T(8,128)(2,1)S(1)}, bf16[2,64,3200]{2,1,0:T(8,128)(2,1)}, u32[]{:S(2)}) copy-start(bf16[2,64,3200]{2,1,0:T(8,128)(2,1)} %param.13) | copy-start | bytes 2457604
  545.0 360.3 %copy-start.6 = (bf16[2,64,3200]{2,1,0:T(8,128)(2,1)S(1)}, bf16[2,64,3200]{2,1,0:T(8,128)(2,1)}, u32[]{:S(2)}) copy-start(bf16[2,64,3200]{2,1,0:T(8,128)(2,1)} %param.14) | copy-start | bytes 2457604
  624.9 280.4 %copy-start.7 = (bf16[64,3200]{1,0:T(8,128)(2,1)S(1)}, bf16[64,3200]{1,0:T(8,128)(2,1)}, u32[]{:S(2)}) copy-start(bf16[64,3200]{1,0:T(8,128)(2,1)} %reduce-scatter.11.cloned.1.call-done) | copy-start | bytes 1228804
  704.9 200.4 %copy-start.8 = (bf16[64,3200]{1,0:T(8,128)(2,1)S(1)}, bf16[64,3200]{1,0:T(8,128)(2,1)}, u32[]{:S(2)}) copy-start(bf16[64,3200]{1,0:T(8,128)(2,1)} %reduce-scatter.13.cloned.1.call-done) | copy-start | bytes 1228804
  900.3 5.0 copy-start.9
  900.3 5.0 copy-start.10
  900.3 5.0 copy-start.11
  900.4 5.0 copy-start.12
  900.4 5.0 copy-start.13
  900.4 5.7 copy-start.14
  (1 other events, 0.7 us)
Sparse Core Ops, SparseCore 0:
  10.8 45.5 all-gather.12
  59.2 42.6 all-gather.14
  104.7 42.6 all-gather.16
  150.1 42.6 all-gather.20
  195.5 42.6 all-gather.22
  240.9 42.6 all-gather.18
  393.3 74.5 reduce-scatter.14
  470.2 76.1 reduce-scatter.16
  548.7 76.1 reduce-scatter.10
  627.0 77.8 reduce-scatter.12
  707.2 75.0 reduce-scatter.6
  784.4 77.1 reduce-scatter.8
where the time goes:
time: 925 us; the launch traced here: 917 us
  waiting for transfers between devices  446 us (48%)
  matrix products  373 us (40%)
  blocking collectives  33.9 us (4%)
  other arithmetic  23.5 us (3%)
  local copies, waits for them, and re-layouts  22.7 us (2%)
  between operations  17.3 us (2%)
    reduce_scatter x6, waiting for transfers between devices, step(): lax.psum_scatter(by_w[name], 'dp', scatter_dimension=0, tiled=True)  312 us
    dot_general x5, matrix products, layer(): gate = jnp.dot(a, w['w_gate'], preferred_element_type=jnp.float32)  137 us
    all_gather x6, waiting for transfers between devices, fetched(): lax.all_gather(w[number], 'dp', axis=0, tiled=True)  132 us
    dot_general x5, matrix products, layer(): up = jnp.dot(a, w['w_up'], preferred_element_type=jnp.float32)  126 us
    dot_general x5, matrix products, matmul(): jnp.dot(a, w, preferred_element_type=jnp.float32).astype(jnp.bfloat16)  110 us
    psum x1, blocking collectives, step(): squares = lax.psum(sum((jnp.sum(g * g) for g in gradients)), 'dp')  33.9 us
  transfers between devices with their start and end apart: 12, of which 11 were waited for; matrix products, arithmetic and copies ran while one was open for 32% of the time, Pallas kernels for 0%

commit v1 on v0

v1 whole, which is shorter than its diff:
```python
import functools

import jax
import jax.numpy as jnp
from jax import lax
from jax.experimental import pallas as pl
from jax.experimental.pallas import tpu as pltpu
from jax.sharding import PartitionSpec as P

BF, F32 = jnp.bfloat16, jnp.float32
ALL = pl.BlockSpec(memory_space=pl.ANY)
DMA = pltpu.SemaphoreType.DMA


def position():
    me = lax.axis_index("dp")
    return [(me // w) % 2 for w in (8, 4, 2, 1)], me


def across(bits, me, axis):
    w = (8, 4, 2, 1)[axis]
    return {"dp": me + w - 2 * w * bits[axis]}


def greet(bits, me):
    barrier = pltpu.get_barrier_semaphore()
    for axis in range(4):
        pl.semaphore_signal(barrier, inc=1, device_id=across(bits, me, axis), device_id_type=pl.DeviceIdType.MESH)
    pl.semaphore_wait(barrier, 4)


def parts_of(columns, pieces):
    lanes, n = columns // 128, 3 * pieces
    cuts = [128 * (lanes * i // n) for i in range(n + 1)]
    return [[(cuts[3 * j + p], cuts[3 * j + p + 1] - cuts[3 * j + p], ((0, 1, 2), (1, 2, 0), (2, 0, 1))[p]) for p in range(3)] for j in range(pieces)]


class Gather:
    def __init__(self, source, layer):
        self.source, self.layer = source, layer
        self.rows, self.columns = source.shape[1:]
        self.parts = parts_of(self.columns, 1)[0]
        self.inputs = [source]
        self.outputs = [jax.ShapeDtypeStruct((2, 2, 2, 2, self.rows, self.columns), BF)]
        self.out_specs = [ALL]
        self.scratch = [pltpu.VMEM((self.rows, self.columns), BF), DMA((2,)), DMA((3, 3)), DMA((3, 3)), DMA((10,)), DMA((10,))]

    def phases(self, inputs, outputs, scratch):
        (source,), (out,), (own, local, send, recv, csend, crecv) = inputs, outputs, scratch
        bits, me = position()

        def region(flipped, both):
            return tuple(slice(None) if a in both else (1 - bits[a] if a in flipped else bits[a]) for a in range(4))

        def hop(stage, p):
            c0, n, order = self.parts[p]
            where = region((), order[:stage]) + (slice(None), pl.ds(c0, n))
            src = own.at[:, pl.ds(c0, n)] if stage == 0 else out.at[where]
            return pltpu.make_async_remote_copy(src, out.at[where], send.at[stage, p], recv.at[stage, p], device_id=across(bits, me, order[stage]), device_id_type=pl.DeviceIdType.MESH)

        def pass_on(stage, p):
            if stage < 0:
                where, src, slot = region((), ()), own, 9
            else:
                c0, n, order = self.parts[p]
                where = region((order[stage],), order[:stage]) + (slice(None), pl.ds(c0, n))
                src, slot = out.at[where], 3 * stage + p
            return pltpu.make_async_remote_copy(src, out.at[where], csend.at[slot], crecv.at[slot], device_id=across(bits, me, 3), device_id_type=pl.DeviceIdType.MESH)

        load = pltpu.make_async_copy(source.at[self.layer], own, local.at[0])
        store = pltpu.make_async_copy(own, out.at[tuple(bits)], local.at[1])

        def first():
            load.start()
            greet(bits, me)
            load.wait()
            for p in range(3):
                hop(0, p).start()
            store.start()
            pass_on(-1, 0).start()

        def middle(stage):
            if stage == 1:
                store.wait()
            for p in range(3):
                hop(stage - 1, p).wait_recv()
                if stage < 3:
                    hop(stage, p).start()
                pass_on(stage - 1, p).start()

        def last():
            for stage in range(3):
                for p in range(3):
                    hop(stage, p).wait_send()
                    pass_on(stage, p).wait()
            pass_on(-1, 0).wait()

        return [first] + [functools.partial(middle, s) for s in (1, 2, 3)] + [last]


class Scatter:
    def __init__(self, g, pieces=2):
        self.rows, self.columns = g.shape[4:]
        self.pieces = parts_of(self.columns, pieces)
        self.inputs = [g]
        r, c, n = self.rows, self.columns, pieces
        self.outputs = [jax.ShapeDtypeStruct((r, c), BF)]
        self.out_specs = [pl.BlockSpec((r, c), lambda *_: (0, 0))]
        buffers = [(2, 2, 2, r, c), (2, 2, 2, r, c), (2, 2, r, c), (2, r, c), (r, c), (2, 2, r, c), (2, r, c), (r, c)]
        self.scratch = [pltpu.VMEM(b, BF) for b in buffers] + [DMA((n,)), DMA((n, 2)), DMA((n, 3, 3)), DMA((n, 3, 3))]

    def phases(self, inputs, outputs, scratch):
        (g,), (out,) = inputs, outputs
        keep, far, in1, in2, in3, out1, out2, out3, local, core, send, recv = scratch
        ins, outs = (in1, in2, in3), (out1, out2, out3)
        bits, me = position()

        def columns_of(j):
            parts = self.pieces[j]
            return pl.ds(parts[0][0], sum(n for _, n, _ in parts))

        def load(j):
            at = columns_of(j)
            return pltpu.make_async_copy(g.at[:, :, :, bits[3], :, at], keep.at[:, :, :, :, at], local.at[j])

        def swap(j):
            at = columns_of(j)
            return pltpu.make_async_remote_copy(g.at[:, :, :, 1 - bits[3], :, at], far.at[:, :, :, :, at], core.at[j, 0], core.at[j, 1], device_id=across(bits, me, 3), device_id_type=pl.DeviceIdType.MESH)

        def hop(j, p, stage):
            c0, n, order = self.pieces[j][p]
            at = (slice(None),) * (2 - stage) + (slice(None), pl.ds(c0, n))
            return pltpu.make_async_remote_copy(outs[stage].at[at], ins[stage].at[at], send.at[j, p, stage], recv.at[j, p, stage], device_id=across(bits, me, order[stage]), device_id_type=pl.DeviceIdType.MESH)

        def total(part, stage, block):
            c0, n, order = part
            at = pl.ds(c0, n)
            xyz = [None] * 3
            for a, b in zip(order, block):
                xyz[a] = b
            where = tuple(xyz) + (slice(None), at)
            t = keep[where].astype(F32) + far[where].astype(F32)
            for s in range(stage):
                t = t + ins[s][tuple(block[s + 1 :]) + (slice(None), at)].astype(F32)
            return t

        def first():
            greet(bits, me)
            for j in range(len(self.pieces)):
                swap(j).start()
                load(j).start()

        def stage_of(j, stage):
            if stage == 0:
                load(j).wait()
                swap(j).wait_recv()
            for p, part in enumerate(self.pieces[j]):
                c0, n, order = part
                b = [bits[a] for a in order]
                if stage:
                    hop(j, p, stage - 1).wait_recv()
                if stage == 3:
                    out[:, pl.ds(c0, n)] = total(part, 3, b).astype(BF)
                    continue
                if stage == 2:
                    out3[:, pl.ds(c0, n)] = total(part, 2, b[:2] + [1 - b[2]]).astype(BF)
                else:
                    @pl.loop(0, 4 if stage == 0 else 2)
                    def _(i):
                        rest = [i // 2, i % 2] if stage == 0 else [i]
                        block = b[:stage] + [1 - b[stage]] + rest
                        outs[stage][tuple(rest) + (slice(None), pl.ds(c0, n))] = total(part, stage, block).astype(BF)
                hop(j, p, stage).start()

        def last():
            for j in range(len(self.pieces)):
                swap(j).wait_send()
                for p in range(3):
                    for stage in range(3):
                        hop(j, p, stage).wait_send()

        middle = [functools.partial(stage_of, j, s) for s in range(4) for j in range(len(self.pieces))]
        return [first] + middle + [last]


def kernel(name, number, grid, compute, inputs, in_specs, outputs, out_specs, scratch=(), comm=None, schedule=(), flops=0, bytes_accessed=0):
    n_in, n_out = len(inputs), len(outputs)
    c_in, c_out, c_scratch = (comm.inputs, comm.outputs, comm.scratch) if comm else ([], [], [])

    def body(*refs):
        step = pl.program_id(0)
        i, o = refs[:n_in], refs[n_in + len(c_in) : n_in + len(c_in) + n_out]
        rest = refs[n_in + len(c_in) + n_out + len(c_out) :]
        phases = []
        if comm:
            phases = comm.phases(refs[n_in : n_in + len(c_in)], refs[n_in + len(c_in) + n_out :][: len(c_out)], rest[len(scratch) :])
        for k, phase in enumerate(phases):
            if k < len(schedule):
                pl.when(step == schedule[k])(phase)
        if compute:
            compute(step, i, o, rest[: len(scratch)])
        if len(phases) > len(schedule):
            @pl.when(step == grid - 1)
            def _():
                for phase in phases[len(schedule) :]:
                    phase()

    return pl.pallas_call(
        body,
        grid=(grid,),
        out_shape=list(outputs) + c_out,
        in_specs=list(in_specs) + [ALL] * len(c_in),
        out_specs=list(out_specs) + (comm.out_specs if comm else []),
        scratch_shapes=list(scratch) + c_scratch,
        compiler_params=pltpu.CompilerParams(
            dimension_semantics=("arbitrary",),
            collective_id=number if comm else None,
            has_side_effects=bool(comm),
            vmem_limit_bytes=60 << 20,
        ),
        cost_estimate=pl.CostEstimate(flops=flops, bytes_accessed=bytes_accessed, transcendentals=0),
        name=name,
    )(*inputs, *c_in)
NAMES = ("w_gate", "w_up", "w_down")
TILE = 256
TURNED = (((1,), (1,)), ((), ()))
SUMMED = (((0,), (0,)), ((), ()))


def chunks(n, size=768):
    starts = list(range(0, n - size + 1, size))
    return [(s, (n if s == starts[-1] else s + size) - s) for s in starts]


def dot(a, b):
    return jnp.dot(a, b, preferred_element_type=F32)


def dot_turned(a, b):
    return lax.dot_general(a, b, TURNED, preferred_element_type=F32)


def rows(columns):
    return pl.BlockSpec((TILE, columns), lambda s: (s, 0))


def whole(shape):
    return pl.BlockSpec(shape, lambda s: (0, 0), pipeline_mode=pl.Buffered(1))


def gate_kernel(number, h, w, comm=None, schedule=()):
    (tokens, d), f = h.shape, w.shape[1]

    def compute(step, i, o, _):
        h_ref, w_ref = i
        a_ref, gate_ref = o
        wide = h_ref[...].astype(F32)
        a = (wide * lax.rsqrt(jnp.mean(wide**2, -1, keepdims=True) + 1e-6)).astype(BF)
        a_ref[...] = a
        for c, n in chunks(f):
            gate_ref[:, c : c + n] = dot(a, w_ref[:, c : c + n])

    outs = [jax.ShapeDtypeStruct((tokens, d), BF), jax.ShapeDtypeStruct((tokens, f), F32)]
    return kernel(f"gate{number}", number, tokens // TILE, compute, [h, w], [rows(d), whole(w.shape)], outs, [rows(d), rows(f)], (), comm, schedule, 2 * tokens * d * f)


def up_kernel(number, a, w, gate, comm=None, schedule=()):
    (tokens, d), f = a.shape, w.shape[1]

    def compute(step, i, o, _):
        a_ref, w_ref, gate_ref = i
        up_ref, act_ref = o
        for c, n in chunks(f):
            at = slice(c, c + n)
            up = dot(a_ref[...], w_ref[:, at])
            up_ref[:, at] = up
            gate = gate_ref[:, at]
            act_ref[:, at] = (gate * jax.nn.sigmoid(gate) * up).astype(BF)

    outs = [jax.ShapeDtypeStruct((tokens, f), F32), jax.ShapeDtypeStruct((tokens, f), BF)]
    return kernel(f"up{number}", number, tokens // TILE, compute, [a, w, gate], [rows(d), whole(w.shape), rows(f)], outs, [rows(f), rows(f)], (), comm, schedule, 2 * tokens * d * f)


def down_kernel(number, act, w, h, comm=None, schedule=()):
    (tokens, f), d = act.shape, w.shape[1]

    def compute(step, i, o, _):
        act_ref, w_ref, h_ref = i
        product = dot(act_ref[...], w_ref[...]).astype(BF)
        o[0][...] = (h_ref[...].astype(F32) + product.astype(F32)).astype(BF)

    outs = [jax.ShapeDtypeStruct((tokens, d), BF)]
    return kernel(f"down{number}", number, tokens // TILE, compute, [act, w, h], [rows(f), whole(w.shape), rows(d)], outs, [rows(d)], (), comm, schedule, 2 * tokens * d * f)


def gated_back(by_act, gate, up):
    s = jax.nn.sigmoid(gate)
    silu = gate * s
    return (by_act * up * (s + silu * (1.0 - s))).astype(BF), (by_act * silu).astype(BF), silu


def hidden_back_kernel(number, by_y, w, comm=None, schedule=()):
    (tokens, d), f = by_y.shape, w.shape[0]

    def compute(step, i, o, _):
        for c, n in chunks(f):
            o[0][:, c : c + n] = dot_turned(i[0][...], i[1][c : c + n, :]).astype(BF)

    outs = [jax.ShapeDtypeStruct((tokens, f), BF)]
    return kernel(f"hidden_back{number}", number, tokens // TILE, compute, [by_y, w], [rows(d), whole(w.shape)], outs, [rows(f)], (), comm, schedule, 2 * tokens * d * f)


def up_back_kernel(number, a, w, gate, by_act, comm=None, schedule=()):
    (tokens, d), f = a.shape, w.shape[1]

    def compute(step, i, o, _):
        a_ref, w_ref, gate_ref, by_ref = i
        act_ref, by_gate_ref, by_up_ref = o
        for c, n in chunks(f):
            at = slice(c, c + n)
            up = dot(a_ref[...], w_ref[:, at])
            by_gate, by_up, silu = gated_back(by_ref[:, at].astype(F32), gate_ref[:, at], up)
            act_ref[:, at], by_gate_ref[:, at], by_up_ref[:, at] = (silu * up).astype(BF), by_gate, by_up

    outs = [jax.ShapeDtypeStruct((tokens, f), BF)] * 3
    return kernel(f"up_back{number}", number, tokens // TILE, compute, [a, w, gate, by_act], [rows(d), whole(w.shape), rows(f), rows(f)], outs, [rows(f)] * 3, (), comm, schedule, 2 * tokens * d * f)


def gated_back_kernel(number, by_y, w, gate, up, comm=None, schedule=()):
    (tokens, d), f = by_y.shape, w.shape[0]

    def compute(step, i, o, _):
        by_ref, w_ref, gate_ref, up_ref = i
        for c, n in chunks(f):
            at = slice(c, c + n)
            by_act = dot_turned(by_ref[...], w_ref[at, :]).astype(BF).astype(F32)
            o[0][:, at], o[1][:, at], _ = gated_back(by_act, gate_ref[:, at], up_ref[:, at])

    outs = [jax.ShapeDtypeStruct((tokens, f), BF)] * 2
    return kernel(f"gated_back{number}", number, tokens // TILE, compute, [by_y, w, gate, up], [rows(d), whole(w.shape), rows(f), rows(f)], outs, [rows(f)] * 2, (), comm, schedule, 2 * tokens * d * f)


def state_back_kernel(number, by_gate, by_up, w_gate, w_up, h, by_y, comm=None, schedule=()):
    (tokens, f), d = by_gate.shape, h.shape[1]

    def compute(step, i, o, _):
        by_gate_ref, by_up_ref, w_gate_ref, w_up_ref, h_ref, by_ref = i
        by_a = dot_turned(by_gate_ref[...], w_gate_ref[...]).astype(BF).astype(F32)
        by_a = (by_a + dot_turned(by_up_ref[...], w_up_ref[...]).astype(BF).astype(F32)).astype(BF).astype(F32)
        wide = h_ref[...].astype(F32)
        scale = lax.rsqrt(jnp.mean(wide**2, -1, keepdims=True) + 1e-6)
        along = jnp.mean(by_a * wide, -1, keepdims=True) * scale * scale * scale
        by_h = (by_a * scale - wide * along).astype(BF)
        o[0][...] = (by_ref[...].astype(F32) + by_h.astype(F32)).astype(BF)

    outs = [jax.ShapeDtypeStruct((tokens, d), BF)]
    specs = [rows(f), rows(f), whole(w_gate.shape), whole(w_up.shape), rows(d), rows(d)]
    return kernel(f"state_back{number}", number, tokens // TILE, compute, [by_gate, by_up, w_gate, w_up, h, by_y], specs, outs, [rows(d)], (), comm, schedule, 4 * tokens * d * f)


def weight_back_kernel(number, x, y, comm=None, schedule=(), tile=640):
    (tokens, m), n = x.shape, y.shape[1]
    if n > m:
        inner = m // 256

        def compute(step, i, o, _):
            at = pl.ds(pl.multiple_of(step % inner * 256, 256), 256)
            o[0][...] = lax.dot_general(i[0][:, at], i[1][...], SUMMED, preferred_element_type=F32).astype(BF)

        grid = n // tile * inner
        specs = [whole(x.shape), pl.BlockSpec((tokens, tile), lambda s: (0, s // inner))]
        out_spec = pl.BlockSpec((256, tile), lambda s: (s % inner, s // inner))
    else:
        tile = 128

        def compute(step, i, o, _):
            o[0][...] = lax.dot_general(i[0][...], i[1][...], SUMMED, preferred_element_type=F32).astype(BF)

        grid = m // tile
        specs = [pl.BlockSpec((tokens, tile), lambda s: (0, s)), whole(y.shape)]
        out_spec = pl.BlockSpec((tile, n), lambda s: (s, 0))
    outs = [jax.ShapeDtypeStruct((m, n), BF)]
    return kernel(f"weight_back{number}", number, grid, compute, [x, y], specs, outs, [out_spec], (), comm, schedule, 2 * tokens * m * n)


class Butterfly:
    def __init__(self, x):
        self.inputs = [x]
        self.outputs = [jax.ShapeDtypeStruct(x.shape, F32)]
        self.out_specs = [pl.BlockSpec(x.shape, lambda *_: (0, 0))]
        self.scratch = [pltpu.VMEM((5,) + x.shape, F32), pltpu.VMEM((4,) + x.shape, F32), DMA((1,)), DMA((4,)), DMA((4,))]

    def phases(self, inputs, outputs, scratch):
        (x,), (out,), (held, arrived, local, send, recv) = inputs, outputs, scratch
        bits, me = position()

        def only():
            load = pltpu.make_async_copy(x, held.at[0], local.at[0])
            load.start()
            greet(bits, me)
            load.wait()
            for k, axis in enumerate((3, 0, 1, 2)):
                copy = pltpu.make_async_remote_copy(held.at[k], arrived.at[k], send.at[k], recv.at[k], device_id=across(bits, me, axis), device_id_type=pl.DeviceIdType.MESH)
                copy.start()
                copy.wait()
                held[k + 1] = held[k] + arrived[k]
            out[...] = held[4]

        return [only]


def adamw(w, m, v, g):
    m = 0.9 * m + 0.1 * g
    v = 0.95 * v + 0.05 * g * g
    step = m * lax.rsqrt(v + 1e-8) + 0.1 * w
    return (w - 0.02 * step).astype(BF), m, v


def clipped(gradients, sum_of_squares, count):
    factor = jnp.minimum(1.0, 0.5 * lax.rsqrt(sum_of_squares / count + 1e-30))
    return [g * factor for g in gradients]


FETCH = (0, 3, 7)
SUM = (0, 4, 7, 12, 17)
SUM8 = (0, 2, 3, 5, 7)


def solution(mesh):
    def cut(g):
        return g.reshape(2, 2, 2, 2, g.shape[0] // 16, g.shape[1])

    def joined(w):
        return w.reshape(-1, w.shape[-1])

    def step(x, dy, *arrays):
        weights, m, v = (arrays[i : i + 3] for i in (0, 3, 6))
        gates, ups, downs = weights
        h0, by_y = x[0], dy[0]
        (g0,) = kernel("fetch", 1, 1, None, [], [], [], [], comm=Gather(gates, 0))
        g0 = joined(g0)
        a0, gate0, u0 = gate_kernel(2, h0, g0, Gather(ups, 0), FETCH)
        up0, act0, d0 = up_kernel(3, a0, joined(u0), gate0, Gather(downs, 0), FETCH)
        h1, g1 = down_kernel(4, act0, joined(d0), h0, Gather(gates, 1), FETCH)
        g1 = joined(g1)
        a1, gate1, d1 = gate_kernel(5, h1, g1, Gather(downs, 1), FETCH)
        by_act1, u1 = hidden_back_kernel(6, by_y, joined(d1), Gather(ups, 1), FETCH)
        u1 = joined(u1)
        act1, by_gate1, by_up1 = up_back_kernel(7, a1, u1, gate1, by_act1)
        (by_d1,) = weight_back_kernel(8, act1, by_y)
        by_g1, sum_d1 = weight_back_kernel(9, a1, by_gate1, Scatter(cut(by_d1)), SUM)
        (by_u1,) = weight_back_kernel(10, a1, by_up1)
        by_h1, sum_g1 = state_back_kernel(11, by_gate1, by_up1, g1, u1, h1, by_y, Scatter(cut(by_g1)), SUM8)
        by_gate0, by_up0, sum_u1 = gated_back_kernel(12, by_h1, joined(d0), gate0, up0, Scatter(cut(by_u1)), SUM8)
        (by_d0,) = weight_back_kernel(13, act0, by_h1)
        by_g0, sum_d0 = weight_back_kernel(14, a0, by_gate0, Scatter(cut(by_d0)), SUM)
        by_u0, sum_g0 = weight_back_kernel(15, a0, by_up0, Scatter(cut(by_g0)), SUM)
        (sum_u0,) = kernel("add", 16, 1, None, [], [], [], [], comm=Scatter(cut(by_u0), 3))
        gradients = [jnp.stack(pair).astype(F32) for pair in ((sum_g0, sum_g1), (sum_u0, sum_u1), (sum_d0, sum_d1))]
        squares = sum(jnp.sum(g * g) for g in gradients)
        (squares,) = kernel("squares", 17, 1, None, [], [], [], [], comm=Butterfly(jnp.broadcast_to(squares, (8, 128))))
        gradients = clipped(gradients, squares[0, 0], 16 * sum(g.size for g in gradients))
        new = [adamw(w.astype(F32), m, v, g) for w, m, v, g in zip(weights, m, v, gradients, strict=True)]
        return tuple(one[which] for which in range(3) for one in new)

    states, block = P(("rep", "dp"), None, None), P(None, "dp", None)
    return jax.shard_map(
        step,
        mesh=mesh,
        in_specs=(states, states) + (block,) * 9,
        out_specs=(P("rep", "dp", None),) * 9,
        check_vma=False,
    )
```

time: 925 us -> 624 us (0.67)
  Pallas kernels: 0 us -> 601 us
  waiting for transfers between devices: 446 us -> 0 us
  matrix products: 373 us -> 0 us
  blocking collectives: 33.9 us -> 0 us
  local copies, waits for them, and re-layouts: 22.7 us -> 3.22 us
  between operations: 17.3 us -> 3.55 us
  other arithmetic: 23.5 us -> 13.3 us
    pallas_call x0 -> x17, Pallas kernels: none -> 601 us  [kernel(): pl.pallas_call(body, grid=(grid,), out_shape=list(outputs) + c_out, in_sp...]
    dot_general x15 -> x0, matrix products: 373 us -> none  [the longest x5 137 us: layer(): gate = jnp.dot(a, w['w_gate'], preferred_element_type=jnp.float32)]
    reduce_scatter x6 -> x0, waiting for transfers between devices: 312 us -> none  [step(): lax.psum_scatter(by_w[name], 'dp', scatter_dimension=0, tiled=True)]
    all_gather x6 -> x0, waiting for transfers between devices: 132 us -> none  [fetched(): lax.all_gather(w[number], 'dp', axis=0, tiled=True)]
    psum x1 -> x0, blocking collectives: 33.9 us -> none  [step(): squares = lax.psum(sum((jnp.sum(g * g) for g in gradients)), 'dp')]
    unnamed x44 -> x28, local copies, waits for them, and re-layouts: 16.5 us -> 1.44 us
  transfers between devices with their start and end apart: 12 -> 0, of which waited for: 11 -> 0; matrix products, arithmetic and copies ran while one was open for 32% -> 0% of each run, Pallas kernels for 0% -> 0%
where the time goes in v1:
time: 624 us; the launch traced here: 621 us
  Pallas kernels  601 us (96%)
  other arithmetic  13.3 us (2%)
    pallas_call x17, Pallas kernels, kernel(): pl.pallas_call(body, grid=(grid,), out_shape=list(outputs) + c_out, in_sp...  601 us

profile of v1, /device:TPU:0, one launch (start us, length us, event | category | flops | bytes accessed | tf_op | source)
XLA Modules:
  0.0 621.2 jit_solution(8862899812081114341)
XLA Ops:
  0.6 32.1 %fetch.1 = bf16[2,2,2,2,64,3200]{5,4,3,2,1,0:T(8,128)(2,1)} custom-call(bf16[2,64,3200]{2,1,0:T(8,128)(2,1)} %refs_3_.3), custom_call_target="tpu_custom_call" | custom-call | tf_op jit(solution)/shard_map/fetch/pallas_call | solution.py:208
  32.8 37.5 %gate2.1 = (bf16[2048,1024]{1,0:T(8,128)(2,1)}, f32[2048,3200]{1,0:T(8,128)}, bf16[2,2,2,2,64,3200]{5,4,3,2,1,0:T(8,128)(2,1)}) custom-call(bf16[2048,1024]{1,0:T(8,128)(2,1)} %bitcast.40, bf16[1024,3200]{1,0:T(8,128)(2,1)} %bitcast.27, bf16[2,64,3200]{2,1,0:T(8,128)(2,1)} %refs_2_.5), custom_call_target="tpu_custom_call" | custom-call | flops 13421772800 | tf_op jit(solution)/shard_map/gate2/pallas_call | solution.py:208
  70.3 48.3 %up3.1 = (f32[2048,3200]{1,0:T(8,128)}, bf16[2048,3200]{1,0:T(8,128)(2,1)}, bf16[2,2,2,2,200,1024]{5,4,3,2,1,0:T(8,128)(2,1)}) custom-call(bf16[2048,1024]{1,0:T(8,128)(2,1)} %get-tuple-element.36.refs_0_, bf16[1024,3200]{1,0:T(8,128)(2,1)} %bitcast.50, f32[2048,3200]{1,0:T(8,128)} %get-tuple-element.38.refs_2_, bf16[2,200,1024]{2,1,0:T(8,128)(2,1)} %refs_2_.4), custom_call_target="tpu_custom_call" | custom-call | flops 13421772800 | tf_op jit(solution)/shard_map/up3/pallas_call | solution.py:208
  118.7 36.8 %down4.1 = (bf16[2048,1024]{1,0:T(8,128)(2,1)}, bf16[2,2,2,2,64,3200]{5,4,3,2,1,0:T(8,128)(2,1)}) custom-call(bf16[2048,3200]{1,0:T(8,128)(2,1)} %get-tuple-element.39.refs_0_, bf16[3200,1024]{1,0:T(8,128)(2,1)} %bitcast.21, bf16[2048,1024]{1,0:T(8,128)(2,1)} %bitcast.41, bf16[2,64,3200]{2,1,0:T(8,128)(2,1)} %refs_3_.3), custom_call_target="tpu_custom_call" | custom-call | flops 13421772800 | tf_op jit(solution)/shard_map/down4/pallas_call | solution.py:208
  155.4 39.3 %gate5.1 = (bf16[2048,1024]{1,0:T(8,128)(2,1)}, f32[2048,3200]{1,0:T(8,128)}, bf16[2,2,2,2,200,1024]{5,4,3,2,1,0:T(8,128)(2,1)}) custom-call(bf16[2048,1024]{1,0:T(8,128)(2,1)} %get-tuple-element.41.refs_0_.refs_4_, bf16[1024,3200]{1,0:T(8,128)(2,1)} %bitcast.45, bf16[2,200,1024]{2,1,0:T(8,128)(2,1)} %refs_2_.4), custom_call_target="tpu_custom_call" | custom-call | flops 13421772800 | tf_op jit(solution)/shard_map/gate5/pallas_call | solution.py:208
  194.8 36.3 %hidden_back6.1 = (bf16[2048,3200]{1,0:T(8,128)(2,1)}, bf16[2,2,2,2,64,3200]{5,4,3,2,1,0:T(8,128)(2,1)}) custom-call(bf16[2048,1024]{1,0:T(8,128)(2,1)} %bitcast.42, bf16[3200,1024]{1,0:T(8,128)(2,1)} %bitcast.51, bf16[2,64,3200]{2,1,0:T(8,128)(2,1)} %refs_2_.5), custom_call_target="tpu_custom_call" | custom-call | flops 13421772800 | tf_op jit(solution)/shard_map/hidden_back6/pallas_call | solution.py:208
  231.1 38.7 %up_back7.1 = (bf16[2048,3200]{1,0:T(8,128)(2,1)}, bf16[2048,3200]{1,0:T(8,128)(2,1)}, bf16[2048,3200]{1,0:T(8,128)(2,1)}) custom-call(bf16[2048,1024]{1,0:T(8,128)(2,1)} %get-tuple-element.43.refs_0_, bf16[1024,3200]{1,0:T(8,128)(2,1)} %bitcast.23, f32[2048,3200]{1,0:T(8,128)} %get-tuple-element.46.refs_2_, bf16[2048,3200]{1,0:T(8,128)(2,1)} %get-tuple-element.47.refs_3_), custom_call_target="tpu_custom_call" | custom-call | flops 13421772800 | tf_op jit(solution)/shard_map/up_back7/pallas_call | solution.py:208
  269.8 26.8 %weight_back8.1 = bf16[3200,1024]{1,0:T(8,128)(2,1)} custom-call(bf16[2048,3200]{1,0:T(8,128)(2,1)} %get-tuple-element.50.refs_0_, bf16[2048,1024]{1,0:T(8,128)(2,1)} %bitcast.43), custom_call_target="tpu_custom_call" | custom-call | flops 13421772800 | tf_op jit(solution)/shard_map/weight_back8/pallas_call | solution.py:208
  296.6 41.0 %weight_back9.1 = (bf16[1024,3200]{1,0:T(8,128)(2,1)}, bf16[200,1024]{1,0:T(8,128)(2,1)}) custom-call(bf16[2048,1024]{1,0:T(8,128)(2,1)} %get-tuple-element.43.refs_0_, bf16[2048,3200]{1,0:T(8,128)(2,1)} %get-tuple-element.48.refs_1_.refs_0_, bf16[2,2,2,2,200,1024]{5,4,3,2,1,0:T(8,128)(2,1)} %bitcast.52), custom_call_target="tpu_custom_call" | custom-call | flops 13421772800 | tf_op jit(solution)/shard_map/weight_back9/pallas_call | solution.py:208
  337.6 48.6 %state_back11.1 = (bf16[2048,1024]{1,0:T(8,128)(2,1)}, bf16[64,3200]{1,0:T(8,128)(2,1)}) custom-call(bf16[2048,3200]{1,0:T(8,128)(2,1)} %get-tuple-element.48.refs_1_.refs_0_, bf16[2048,3200]{1,0:T(8,128)(2,1)} %get-tuple-element.49.refs_1_, bf16[1024,3200]{1,0:T(8,128)(2,1)} %bitcast.46, bf16[1024,3200]{1,0:T(8,128)(2,1)} %bitcast.24, ...), custom_call_target="tpu_custom_call" | custom-call | flops 26843545600 | tf_op jit(solution)/shard_map/state_back11/pallas_call | solution.py:208
  386.2 28.1 %weight_back10.1 = bf16[1024,3200]{1,0:T(8,128)(2,1)} custom-call(bf16[2048,1024]{1,0:T(8,128)(2,1)} %get-tuple-element.43.refs_0_, bf16[2048,3200]{1,0:T(8,128)(2,1)} %get-tuple-element.49.refs_1_), custom_call_target="tpu_custom_call" | custom-call | flops 13421772800 | tf_op jit(solution)/shard_map/weight_back10/pallas_call | solution.py:208
  414.3 26.8 %weight_back13.1 = bf16[3200,1024]{1,0:T(8,128)(2,1)} custom-call(bf16[2048,3200]{1,0:T(8,128)(2,1)} %get-tuple-element.39.refs_0_, bf16[2048,1024]{1,0:T(8,128)(2,1)} %get-tuple-element.52.refs_0_.refs_1_), custom_call_target="tpu_custom_call" | custom-call | flops 13421772800 | tf_op jit(solution)/shard_map/weight_back13/pallas_call | solution.py:208
  441.1 44.8 %gated_back12.1 = (bf16[2048,3200]{1,0:T(8,128)(2,1)}, bf16[2048,3200]{1,0:T(8,128)(2,1)}, bf16[64,3200]{1,0:T(8,128)(2,1)}) custom-call(bf16[2048,1024]{1,0:T(8,128)(2,1)} %get-tuple-element.52.refs_0_.refs_1_, bf16[3200,1024]{1,0:T(8,128)(2,1)} %bitcast.22, f32[2048,3200]{1,0:T(8,128)} %get-tuple-element.38.refs_2_, ...), custom_call_target="tpu_custom_call" | custom-call | flops 13421772800 | tf_op jit(solution)/shard_map/gated_back12/pallas_call | solution.py:208
  485.9 40.7 %weight_back14.1 = (bf16[1024,3200]{1,0:T(8,128)(2,1)}, bf16[200,1024]{1,0:T(8,128)(2,1)}) custom-call(bf16[2048,1024]{1,0:T(8,128)(2,1)} %get-tuple-element.36.refs_0_, bf16[2048,3200]{1,0:T(8,128)(2,1)} %get-tuple-element.55.refs_1_, bf16[2,2,2,2,200,1024]{5,4,3,2,1,0:T(8,128)(2,1)} %bitcast.47), custom_call_target="tpu_custom_call" | custom-call | flops 13421772800 | tf_op jit(solution)/shard_map/weight_back14/pallas_call | solution.py:208
  526.7 2.0 fusion.11
  528.7 36.5 %weight_back15.1 = (bf16[1024,3200]{1,0:T(8,128)(2,1)}, bf16[64,3200]{1,0:T(8,128)(2,1)}) custom-call(bf16[2048,1024]{1,0:T(8,128)(2,1)} %get-tuple-element.36.refs_0_, bf16[2048,3200]{1,0:T(8,128)(2,1)} %get-tuple-element.54.refs_1_, bf16[2,2,2,2,64,3200]{5,4,3,2,1,0:T(8,128)(2,1)} %bitcast.49), custom_call_target="tpu_custom_call" | custom-call | flops 13421772800 | tf_op jit(solution)/shard_map/weight_back15/pallas_call | solution.py:208
  565.2 0.0 copy-start.3
  565.2 28.4 %add.103 = bf16[64,3200]{1,0:T(8,128)(2,1)} custom-call(bf16[2,2,2,2,64,3200]{5,4,3,2,1,0:T(8,128)(2,1)} %bitcast.26), custom_call_target="tpu_custom_call" | custom-call | tf_op jit(solution)/shard_map/add/pallas_call | solution.py:208
  593.7 0.0 copy-start.2
  593.7 2.4 fusion.9
  598.0 0.6 broadcast_in_dim.3.refs_0_
  598.6 10.3 %squares.1 = f32[8,128]{1,0:T(8,128)} custom-call(f32[8,128]{1,0:T(8,128)} %broadcast_in_dim.3.refs_0_), custom_call_target="tpu_custom_call" | custom-call | tf_op jit(solution)/shard_map/squares/pallas_call | solution.py:208
  608.9 1.2 slice.3
  610.8 0.0 copy-start.1
  610.8 0.0 copy-start.4
  610.9 4.0 fusion.17
  614.9 0.0 copy-start.6
  615.0 2.4 fusion.8
  617.4 1.0 copy-done.7
  618.5 0.1 copy-done.10
  618.5 0.3 copy-done.13
  618.8 2.4 fusion.14
  (20 shorter events, 0.0 us)
Async XLA Ops:
  485.9 40.8 %copy-start.12 = (bf16[200,1024]{1,0:T(8,128)(2,1)S(1)}, bf16[200,1024]{1,0:T(8,128)(2,1)}, u32[]{:S(2)}) copy-start(bf16[200,1024]{1,0:T(8,128)(2,1)} %get-tuple-element.62) | copy-start | bytes 1228804
  565.2 28.5 %copy-start.8 = (bf16[64,3200]{1,0:T(8,128)(2,1)S(1)}, bf16[64,3200]{1,0:T(8,128)(2,1)}, u32[]{:S(2)}) copy-start(bf16[64,3200]{1,0:T(8,128)(2,1)} %get-tuple-element.58) | copy-start | bytes 1228804
  565.2 45.6 %copy-start.3 = (f32[2,200,1024]{2,1,0:T(8,128)S(1)}, f32[2,200,1024]{2,1,0:T(8,128)}, u32[]{:S(2)}) copy-start(f32[2,200,1024]{2,1,0:T(8,128)} %param.18) | copy-start | bytes 4915204
  593.7 17.2 %copy-start.2 = (f32[2,200,1024]{2,1,0:T(8,128)S(1)}, f32[2,200,1024]{2,1,0:T(8,128)}, u32[]{:S(2)}) copy-start(f32[2,200,1024]{2,1,0:T(8,128)} %param.21) | copy-start | bytes 4915204
  610.8 4.1 copy-start.1
  610.8 4.1 copy-start.4
  610.9 4.1 copy-start.5
  610.9 4.1 copy-start.9
  610.9 4.1 copy-start.11
  614.9 2.5 copy-start
  614.9 2.5 copy-start.6
  615.0 3.5 copy-start.7
  615.0 3.6 copy-start.10
  615.0 3.8 copy-start.13

commit v2 on v1

v2 whole, which is shorter than its diff:
```python
import functools

import jax
import jax.numpy as jnp
from jax import lax
from jax.experimental import pallas as pl
from jax.experimental.pallas import tpu as pltpu
from jax.sharding import PartitionSpec as P

BF, F32 = jnp.bfloat16, jnp.float32
ALL = pl.BlockSpec(memory_space=pl.ANY)
DMA = pltpu.SemaphoreType.DMA


def position():
    me = lax.axis_index("dp")
    return [(me // w) % 2 for w in (8, 4, 2, 1)], me


def across(bits, me, axis):
    w = (8, 4, 2, 1)[axis]
    return {"dp": me + w - 2 * w * bits[axis]}


def greet(bits, me):
    barrier = pltpu.get_barrier_semaphore()
    for axis in range(4):
        pl.semaphore_signal(barrier, inc=1, device_id=across(bits, me, axis), device_id_type=pl.DeviceIdType.MESH)
    pl.semaphore_wait(barrier, 4)


ORDERS = ((0, 1, 2), (1, 2, 0), (2, 0, 1))


def parts_of(columns, pieces):
    lanes, start, result = columns // 128, 0, []
    for j in range(pieces):
        piece = []
        for p, order in enumerate(ORDERS):
            mine = (lanes + 2 - p) // 3
            n = 128 * (mine * (j + 1) // pieces - mine * j // pieces)
            if n:
                piece.append((start, n, order))
            start += n
        result.append(piece)
    return result


class Gather:
    def __init__(self, source, layer, pieces=2):
        self.source, self.layer = source, layer
        self.rows, self.columns = source.shape[1:]
        self.pieces = parts_of(self.columns, pieces)
        self.inputs = [source]
        self.outputs = [jax.ShapeDtypeStruct((2, 2, 2, 2, self.rows, self.columns), BF)]
        self.out_specs = [ALL]
        n = pieces
        self.scratch = [pltpu.VMEM((self.rows, self.columns), BF), DMA((2,)), DMA((n, 3, 3)), DMA((n, 3, 3)), DMA((n, 3, 3)), DMA((n, 3, 3)), DMA((2,))]

    def phases(self, inputs, outputs, scratch):
        (source,), (out,), (own, local, send, recv, csend, crecv, cown) = inputs, outputs, scratch
        bits, me = position()
        count = len(self.pieces)

        def region(flipped, both):
            return tuple(slice(None) if a in both else (1 - bits[a] if a in flipped else bits[a]) for a in range(4))

        def remote(src, dst, send_sem, recv_sem, axis):
            return pltpu.make_async_remote_copy(src, dst, send_sem, recv_sem, device_id=across(bits, me, axis), device_id_type=pl.DeviceIdType.MESH)

        def hop(j, p, stage):
            c0, n, order = self.pieces[j][p]
            where = region((), order[:stage]) + (slice(None), pl.ds(c0, n))
            src = own.at[:, pl.ds(c0, n)] if stage == 0 else out.at[where]
            return remote(src, out.at[where], send.at[j, p, stage], recv.at[j, p, stage], order[stage])

        def pass_on(j, p, stage):
            c0, n, order = self.pieces[j][p]
            where = region((order[stage],), order[:stage]) + (slice(None), pl.ds(c0, n))
            return remote(out.at[where], out.at[where], csend.at[j, p, stage], crecv.at[j, p, stage], 3)

        load = pltpu.make_async_copy(source.at[self.layer], own, local.at[0])
        store = pltpu.make_async_copy(own, out.at[tuple(bits)], local.at[1])
        give = remote(own, out.at[tuple(bits)], cown.at[0], cown.at[1], 3)

        def first():
            load.start()
            greet(bits, me)
            load.wait()
            for j in range(count):
                for p in range(len(self.pieces[j])):
                    hop(j, p, 0).start()
            store.start()
            give.start()

        def middle(j, stage):
            if stage == 1 and j == 0:
                store.wait()
            for p in range(len(self.pieces[j])):
                hop(j, p, stage - 1).wait_recv()
                if stage < 3:
                    hop(j, p, stage).start()
            for p in range(len(self.pieces[j])):
                pass_on(j, p, stage - 1).start()

        def last():
            give.wait()
            for j in range(count):
                for p in range(len(self.pieces[j])):
                    for stage in range(3):
                        hop(j, p, stage).wait_send()
                        pass_on(j, p, stage).wait()

        return [first] + [functools.partial(middle, j, s) for s in (1, 2, 3) for j in range(count)] + [last]


class Scatter:
    def __init__(self, g, pieces=2):
        self.rows, self.columns = g.shape[4:]
        self.pieces = parts_of(self.columns, pieces)
        self.inputs = [g]
        r, c, n = self.rows, self.columns, pieces
        self.outputs = [jax.ShapeDtypeStruct((r, c), BF)]
        self.out_specs = [pl.BlockSpec((r, c), lambda *_: (0, 0))]
        buffers = [(2, 2, 2, r, c), (2, 2, 2, r, c), (2, 2, r, c), (2, r, c), (r, c), (2, 2, r, c), (2, r, c), (r, c)]
        self.scratch = [pltpu.VMEM(b, BF) for b in buffers] + [DMA((n,)), DMA((n, 2)), DMA((n, 3, 3)), DMA((n, 3, 3))]

    def phases(self, inputs, outputs, scratch):
        (g,), (out,) = inputs, outputs
        keep, far, in1, in2, in3, out1, out2, out3, local, core, send, recv = scratch
        ins, outs = (in1, in2, in3), (out1, out2, out3)
        bits, me = position()

        def columns_of(j):
            parts = self.pieces[j]
            return pl.ds(parts[0][0], sum(n for _, n, _ in parts))

        def load(j):
            at = columns_of(j)
            return pltpu.make_async_copy(g.at[:, :, :, bits[3], :, at], keep.at[:, :, :, :, at], local.at[j])

        def swap(j):
            at = columns_of(j)
            return pltpu.make_async_remote_copy(g.at[:, :, :, 1 - bits[3], :, at], far.at[:, :, :, :, at], core.at[j, 0], core.at[j, 1], device_id=across(bits, me, 3), device_id_type=pl.DeviceIdType.MESH)

        def hop(j, p, stage):
            c0, n, order = self.pieces[j][p]
            at = (slice(None),) * (2 - stage) + (slice(None), pl.ds(c0, n))
            return pltpu.make_async_remote_copy(outs[stage].at[at], ins[stage].at[at], send.at[j, p, stage], recv.at[j, p, stage], device_id=across(bits, me, order[stage]), device_id_type=pl.DeviceIdType.MESH)

        def total(part, stage, block):
            c0, n, order = part
            at = pl.ds(c0, n)
            xyz = [None] * 3
            for a, b in zip(order, block):
                xyz[a] = b
            where = tuple(xyz) + (slice(None), at)
            t = keep[where].astype(F32) + far[where].astype(F32)
            for s in range(stage):
                t = t + ins[s][tuple(block[s + 1 :]) + (slice(None), at)].astype(F32)
            return t

        def first():
            greet(bits, me)
            for j in range(len(self.pieces)):
                swap(j).start()
                load(j).start()

        def stage_of(j, stage):
            if stage == 0:
                load(j).wait()
                swap(j).wait_recv()
            for p, part in enumerate(self.pieces[j]):
                c0, n, order = part
                b = [bits[a] for a in order]
                if stage:
                    hop(j, p, stage - 1).wait_recv()
                if stage == 3:
                    out[:, pl.ds(c0, n)] = total(part, 3, b).astype(BF)
                    continue
                if stage == 2:
                    out3[:, pl.ds(c0, n)] = total(part, 2, b[:2] + [1 - b[2]]).astype(BF)
                else:
                    @pl.loop(0, 4 if stage == 0 else 2)
                    def _(i):
                        rest = [i // 2, i % 2] if stage == 0 else [i]
                        block = b[:stage] + [1 - b[stage]] + rest
                        outs[stage][tuple(rest) + (slice(None), pl.ds(c0, n))] = total(part, stage, block).astype(BF)
                hop(j, p, stage).start()

        def last():
            for j in range(len(self.pieces)):
                swap(j).wait_send()
                for p in range(len(self.pieces[j])):
                    for stage in range(3):
                        hop(j, p, stage).wait_send()

        middle = [functools.partial(stage_of, j, s) for s in range(4) for j in range(len(self.pieces))]
        return [first] + middle + [last]


def kernel(name, number, grid, ticks, compute, inputs, in_specs, outputs, out_specs, scratch=(), comm=None, times=(), length=1.0, flops=0):
    n_in, n_out = len(inputs), len(outputs)
    comms = [] if comm is None else list(comm) if isinstance(comm, (list, tuple)) else [comm]
    c_in, c_out = [x for c in comms for x in c.inputs], [x for c in comms for x in c.outputs]
    c_scratch = [x for c in comms for x in c.scratch]
    total_ticks = grid * ticks

    def body(*refs):
        step = pl.program_id(0)
        i, o = refs[:n_in], refs[n_in + len(c_in) : n_in + len(c_in) + n_out]
        ci, co = list(refs[n_in : n_in + len(c_in)]), list(refs[n_in + len(c_in) + n_out :][: len(c_out)])
        rest = list(refs[n_in + len(c_in) + n_out + len(c_out) :])
        own, cs = rest[: len(scratch)], rest[len(scratch) :]
        phases = []
        for c in comms:
            mine = [[l.pop(0) for _ in range(n)] for l, n in ((ci, len(c.inputs)), (co, len(c.outputs)), (cs, len(c.scratch)))]
            phases += c.phases(*mine)
        when = [-int(-t * total_ticks // length) for t in times][: len(phases)]
        when += [total_ticks] * (len(phases) - len(when))

        def tick(k):
            for phase, w in zip(phases, when):
                if w < total_ticks and w % ticks == k:
                    pl.when(step == w // ticks)(phase)

        if compute:
            compute(step, i, o, own, tick)

        @pl.when(step == grid - 1)
        def _():
            for phase, w in zip(phases, when):
                if w >= total_ticks:
                    phase()

    return pl.pallas_call(
        body,
        grid=(grid,),
        out_shape=list(outputs) + c_out,
        in_specs=list(in_specs) + [ALL] * len(c_in),
        out_specs=list(out_specs) + [s for c in comms for s in c.out_specs],
        scratch_shapes=list(scratch) + c_scratch,
        compiler_params=pltpu.CompilerParams(
            dimension_semantics=("arbitrary",),
            collective_id=number if comms else None,
            has_side_effects=bool(comms),
            vmem_limit_bytes=62 << 20,
        ),
        cost_estimate=pl.CostEstimate(flops=flops, bytes_accessed=0, transcendentals=0),
        name=name,
    )(*inputs, *c_in)
NAMES = ("w_gate", "w_up", "w_down")
TILE = 256
TICKS = 2
TURNED = (((1,), (1,)), ((), ()))
SUMMED = (((0,), (0,)), ((), ()))


def chunks(n, size=768):
    starts = list(range(0, n - size + 1, size))
    return [(s, (n if s == starts[-1] else s + size) - s) for s in starts]


def dot(a, b):
    return jnp.dot(a, b, preferred_element_type=F32)


def dot_turned(a, b):
    return lax.dot_general(a, b, TURNED, preferred_element_type=F32)


def rows(columns):
    return pl.BlockSpec((TILE, columns), lambda s: (s, 0))


def whole(shape):
    return pl.BlockSpec(shape, lambda s: (0, 0), pipeline_mode=pl.Buffered(1))


def gate_kernel(number, h, w, comm=None, times=(), length=20.0):
    (tokens, d), f = h.shape, w.shape[1]

    def compute(step, i, o, _, tick):
        h_ref, w_ref = i
        a_ref, gate_ref = o
        wide = h_ref[...].astype(F32)
        a = (wide * lax.rsqrt(jnp.mean(wide**2, -1, keepdims=True) + 1e-6)).astype(BF)
        a_ref[...] = a
        for k, (c, n) in enumerate(chunks(f)):
            tick(k)
            gate_ref[:, c : c + n] = dot(a, w_ref[:, c : c + n])

    outs = [jax.ShapeDtypeStruct((tokens, d), BF), jax.ShapeDtypeStruct((tokens, f), F32)]
    return kernel(f"gate{number}", number, tokens // TILE, TICKS, compute, [h, w], [rows(d), whole(w.shape)], outs, [rows(d), rows(f)], (), comm, times, length, 2 * tokens * d * f)


def up_kernel(number, a, w, gate, comm=None, times=(), length=20.0):
    (tokens, d), f = a.shape, w.shape[1]

    def compute(step, i, o, _, tick):
        a_ref, w_ref, gate_ref = i
        up_ref, act_ref = o
        for k, (c, n) in enumerate(chunks(f)):
            tick(k)
            at = slice(c, c + n)
            up = dot(a_ref[...], w_ref[:, at])
            up_ref[:, at] = up
            gate = gate_ref[:, at]
            act_ref[:, at] = (gate * sigmoid(gate) * up).astype(BF)

    outs = [jax.ShapeDtypeStruct((tokens, f), F32), jax.ShapeDtypeStruct((tokens, f), BF)]
    return kernel(f"up{number}", number, tokens // TILE, TICKS, compute, [a, w, gate], [rows(d), whole(w.shape), rows(f)], outs, [rows(f), rows(f)], (), comm, times, length, 2 * tokens * d * f)


def down_kernel(number, act, w, h, comm=None, times=(), length=20.0):
    (tokens, f), d = act.shape, w.shape[1]

    def compute(step, i, o, _, tick):
        act_ref, w_ref, h_ref = i
        for k in range(TICKS):
            tick(k)
            at = slice(k * d // TICKS, (k + 1) * d // TICKS)
            product = dot(act_ref[...], w_ref[:, at]).astype(BF)
            o[0][:, at] = (h_ref[:, at].astype(F32) + product.astype(F32)).astype(BF)

    outs = [jax.ShapeDtypeStruct((tokens, d), BF)]
    return kernel(f"down{number}", number, tokens // TILE, TICKS, compute, [act, w, h], [rows(f), whole(w.shape), rows(d)], outs, [rows(d)], (), comm, times, length, 2 * tokens * d * f)


def sigmoid(x):
    return 0.5 * jnp.tanh(0.5 * x) + 0.5


def gated_back(by_act, gate, up):
    s = sigmoid(gate)
    silu = gate * s
    return (by_act * up * (s + silu * (1.0 - s))).astype(BF), (by_act * silu).astype(BF), silu


def hidden_back_kernel(number, by_y, w, comm=None, times=(), length=20.0):
    (tokens, d), f = by_y.shape, w.shape[0]

    def compute(step, i, o, _, tick):
        for k, (c, n) in enumerate(chunks(f)):
            tick(k)
            o[0][:, c : c + n] = dot_turned(i[0][...], i[1][c : c + n, :]).astype(BF)

    outs = [jax.ShapeDtypeStruct((tokens, f), BF)]
    return kernel(f"hidden_back{number}", number, tokens // TILE, TICKS, compute, [by_y, w], [rows(d), whole(w.shape)], outs, [rows(f)], (), comm, times, length, 2 * tokens * d * f)


def up_back_kernel(number, a, w, gate, by_act, comm=None, times=(), length=20.0):
    (tokens, d), f = a.shape, w.shape[1]

    def compute(step, i, o, _, tick):
        a_ref, w_ref, gate_ref, by_ref = i
        act_ref, by_gate_ref, by_up_ref = o
        for k, (c, n) in enumerate(chunks(f)):
            tick(k)
            at = slice(c, c + n)
            up = dot(a_ref[...], w_ref[:, at])
            by_gate, by_up, silu = gated_back(by_ref[:, at].astype(F32), gate_ref[:, at], up)
            act_ref[:, at], by_gate_ref[:, at], by_up_ref[:, at] = (silu * up).astype(BF), by_gate, by_up

    outs = [jax.ShapeDtypeStruct((tokens, f), BF)] * 3
    return kernel(f"up_back{number}", number, tokens // TILE, TICKS, compute, [a, w, gate, by_act], [rows(d), whole(w.shape), rows(f), rows(f)], outs, [rows(f)] * 3, (), comm, times, length, 2 * tokens * d * f)


def gated_back_kernel(number, by_y, w, gate, up, comm=None, times=(), length=20.0):
    (tokens, d), f = by_y.shape, w.shape[0]

    def compute(step, i, o, _, tick):
        by_ref, w_ref, gate_ref, up_ref = i
        for k, (c, n) in enumerate(chunks(f)):
            tick(k)
            at = slice(c, c + n)
            by_act = dot_turned(by_ref[...], w_ref[at, :]).astype(BF).astype(F32)
            o[0][:, at], o[1][:, at], _ = gated_back(by_act, gate_ref[:, at], up_ref[:, at])

    outs = [jax.ShapeDtypeStruct((tokens, f), BF)] * 2
    return kernel(f"gated_back{number}", number, tokens // TILE, TICKS, compute, [by_y, w, gate, up], [rows(d), whole(w.shape), rows(f), rows(f)], outs, [rows(f)] * 2, (), comm, times, length, 2 * tokens * d * f)


def state_back_kernel(number, by_gate, by_up, w_gate, w_up, h, by_y, comm=None, times=(), length=20.0):
    (tokens, f), d = by_gate.shape, h.shape[1]

    def compute(step, i, o, scratch, tick):
        by_gate_ref, by_up_ref, w_gate_ref, w_up_ref, h_ref, by_ref = i
        for k in range(TICKS):
            tick(k)
            at = slice(k * d // TICKS, (k + 1) * d // TICKS)
            part = dot_turned(by_gate_ref[...], w_gate_ref[at, :]).astype(BF).astype(F32)
            part += dot_turned(by_up_ref[...], w_up_ref[at, :]).astype(BF).astype(F32)
            scratch[0][:, at] = part.astype(BF).astype(F32)
        by_a = scratch[0][...]
        wide = h_ref[...].astype(F32)
        scale = lax.rsqrt(jnp.mean(wide**2, -1, keepdims=True) + 1e-6)
        along = jnp.mean(by_a * wide, -1, keepdims=True) * scale * scale * scale
        by_h = (by_a * scale - wide * along).astype(BF)
        o[0][...] = (by_ref[...].astype(F32) + by_h.astype(F32)).astype(BF)

    outs = [jax.ShapeDtypeStruct((tokens, d), BF)]
    specs = [rows(f), rows(f), whole(w_gate.shape), whole(w_up.shape), rows(d), rows(d)]
    return kernel(f"state_back{number}", number, tokens // TILE, TICKS, compute, [by_gate, by_up, w_gate, w_up, h, by_y], specs, outs, [rows(d)], [pltpu.VMEM((TILE, d), F32)], comm, times, length, 4 * tokens * d * f)


def weight_back_kernel(number, x, y, comm=None, times=(), length=20.0, tile=640):
    (tokens, m), n = x.shape, y.shape[1]
    wide = n > m
    tiled, still = (y, x) if wide else (x, y)
    part = still.shape[1] // TICKS

    def compute(step, i, o, _, tick):
        for k in range(TICKS):
            tick(k)
            at = slice(k * part, (k + 1) * part)
            product = lax.dot_general(i[0][...], i[1][:, at], SUMMED, preferred_element_type=F32).astype(BF)
            if wide:
                o[0][at, :] = product.T
            else:
                o[0][:, at] = product

    specs = [pl.BlockSpec((tokens, tile), lambda s: (0, s)), whole(still.shape)]
    out_spec = pl.BlockSpec((m, tile), lambda s: (0, s)) if wide else pl.BlockSpec((tile, n), lambda s: (s, 0))
    outs = [jax.ShapeDtypeStruct((m, n), BF)]
    return kernel(f"weight_back{number}", number, tiled.shape[1] // tile, TICKS, compute, [tiled, still], specs, outs, [out_spec], (), comm, times, length, 2 * tokens * m * n)


class Butterfly:
    def __init__(self, x):
        self.inputs = [x]
        self.outputs = [jax.ShapeDtypeStruct(x.shape, F32)]
        self.out_specs = [pl.BlockSpec(x.shape, lambda *_: (0, 0))]
        self.scratch = [pltpu.VMEM((5,) + x.shape, F32), pltpu.VMEM((4,) + x.shape, F32), DMA((1,)), DMA((4,)), DMA((4,))]

    def phases(self, inputs, outputs, scratch):
        (x,), (out,), (held, arrived, local, send, recv) = inputs, outputs, scratch
        bits, me = position()

        def only():
            load = pltpu.make_async_copy(x, held.at[0], local.at[0])
            load.start()
            greet(bits, me)
            load.wait()
            for k, axis in enumerate((3, 0, 1, 2)):
                copy = pltpu.make_async_remote_copy(held.at[k], arrived.at[k], send.at[k], recv.at[k], device_id=across(bits, me, axis), device_id_type=pl.DeviceIdType.MESH)
                copy.start()
                copy.wait()
                held[k + 1] = held[k] + arrived[k]
            out[...] = held[4]

        return [only]


def adamw(w, m, v, g):
    m = 0.9 * m + 0.1 * g
    v = 0.95 * v + 0.05 * g * g
    step = m * lax.rsqrt(v + 1e-8) + 0.1 * w
    return (w - 0.02 * step).astype(BF), m, v


def clipped(gradients, sum_of_squares, count):
    factor = jnp.minimum(1.0, 0.5 * lax.rsqrt(sum_of_squares / count + 1e-30))
    return [g * factor for g in gradients]


FETCH = (0.0, 4.0, 5.5, 9.0, 12.0, 18.0)
SUM = (0.0, 5.5, 8.0, 14.0, 20.0, 22.0, 25.0, 28.0, 31.0)


def solution(mesh):
    def cut(g):
        return g.reshape(2, 2, 2, 2, g.shape[0] // 16, g.shape[1])

    def joined(w):
        return w.reshape(-1, w.shape[-1])

    def step(x, dy, *arrays):
        weights, m, v = (arrays[i : i + 3] for i in (0, 3, 6))
        gates, ups, downs = weights
        h0, by_y = x[0], dy[0]
        (g0,) = kernel("fetch", 1, 1, 1, None, [], [], [], [], comm=Gather(gates, 0, 3))
        g0 = joined(g0)
        a0, gate0, u0 = gate_kernel(2, h0, g0, Gather(ups, 0), FETCH, 21.0)
        up0, act0, d0 = up_kernel(3, a0, joined(u0), gate0, Gather(downs, 0), FETCH, 31.0)
        h1, g1 = down_kernel(4, act0, joined(d0), h0, Gather(gates, 1), FETCH, 21.0)
        g1 = joined(g1)
        a1, gate1, d1 = gate_kernel(5, h1, g1, Gather(downs, 1), FETCH, 21.0)
        by_act1, u1 = hidden_back_kernel(6, by_y, joined(d1), Gather(ups, 1), FETCH, 20.0)
        u1 = joined(u1)
        act1, by_gate1, by_up1 = up_back_kernel(7, a1, u1, gate1, by_act1)
        (by_d1,) = weight_back_kernel(8, act1, by_y)
        by_g1, sum_d1 = weight_back_kernel(9, a1, by_gate1, Scatter(cut(by_d1)), SUM, 20.0)
        (by_u1,) = weight_back_kernel(10, a1, by_up1)
        by_h1, sum_g1 = state_back_kernel(11, by_gate1, by_up1, g1, u1, h1, by_y, Scatter(cut(by_g1)), SUM, 40.0)
        by_gate0, by_up0, sum_u1 = gated_back_kernel(12, by_h1, joined(d0), gate0, up0, Scatter(cut(by_u1)), SUM, 38.0)
        (by_d0,) = weight_back_kernel(13, act0, by_h1)
        by_g0, sum_d0 = weight_back_kernel(14, a0, by_gate0, Scatter(cut(by_d0)), SUM, 20.0)
        by_u0, sum_g0 = weight_back_kernel(15, a0, by_up0, Scatter(cut(by_g0)), SUM, 20.0)
        (sum_u0,) = kernel("add", 16, 1, 1, None, [], [], [], [], comm=Scatter(cut(by_u0), 3))
        gradients = [jnp.stack(pair).astype(F32) for pair in ((sum_g0, sum_g1), (sum_u0, sum_u1), (sum_d0, sum_d1))]
        squares = sum(jnp.sum(g * g) for g in gradients)
        (squares,) = kernel("squares", 17, 1, 1, None, [], [], [], [], comm=Butterfly(jnp.broadcast_to(squares, (8, 128))))
        gradients = clipped(gradients, squares[0, 0], 16 * sum(g.size for g in gradients))
        new = [adamw(w.astype(F32), m, v, g) for w, m, v, g in zip(weights, m, v, gradients, strict=True)]
        return tuple(one[which] for which in range(3) for one in new)

    states, block = P(("rep", "dp"), None, None), P(None, "dp", None)
    return jax.shard_map(
        step,
        mesh=mesh,
        in_specs=(states, states) + (block,) * 9,
        out_specs=(P("rep", "dp", None),) * 9,
        check_vma=False,
    )
```

time: 624 us -> 573 us (0.918)
  Pallas kernels: 601 us -> 543 us
    pallas_call x17, Pallas kernels: 601 us -> 543 us  [kernel(): pl.pallas_call(body, grid=(grid,), out_shape=list(outputs) + c_out, in_sp...]
where the time goes in v2:
time: 573 us; the launch traced here: 564 us
  Pallas kernels  543 us (95%)
  other arithmetic  14.1 us (2%)
    pallas_call x17, Pallas kernels, kernel(): pl.pallas_call(body, grid=(grid,), out_shape=list(outputs) + c_out, in_sp...  543 us

profile of v2, /device:TPU:0, one launch (start us, length us, event | category | flops | bytes accessed | tf_op | source)
XLA Modules:
  0.0 564.2 jit_solution(1107657378893309146)
XLA Ops:
  0.6 29.3 %fetch.1 = bf16[2,2,2,2,64,3200]{5,4,3,2,1,0:T(8,128)(2,1)} custom-call(bf16[2,64,3200]{2,1,0:T(8,128)(2,1)} %refs_3_.3), custom_call_target="tpu_custom_call" | custom-call | tf_op jit(solution)/shard_map/fetch/pallas_call | solution.py:236
  29.9 34.4 %gate2.1 = (bf16[2048,1024]{1,0:T(8,128)(2,1)}, f32[2048,3200]{1,0:T(8,128)}, bf16[2,2,2,2,64,3200]{5,4,3,2,1,0:T(8,128)(2,1)}) custom-call(bf16[2048,1024]{1,0:T(8,128)(2,1)} %bitcast.40, bf16[1024,3200]{1,0:T(8,128)(2,1)} %bitcast.27, bf16[2,64,3200]{2,1,0:T(8,128)(2,1)} %refs_2_.5), custom_call_target="tpu_custom_call" | custom-call | flops 13421772800 | tf_op jit(solution)/shard_map/gate2/pallas_call | solution.py:236
  64.3 39.8 %up3.1 = (f32[2048,3200]{1,0:T(8,128)}, bf16[2048,3200]{1,0:T(8,128)(2,1)}, bf16[2,2,2,2,200,1024]{5,4,3,2,1,0:T(8,128)(2,1)}) custom-call(bf16[2048,1024]{1,0:T(8,128)(2,1)} %get-tuple-element.36.refs_0_.refs_1_, bf16[1024,3200]{1,0:T(8,128)(2,1)} %bitcast.50, f32[2048,3200]{1,0:T(8,128)} %get-tuple-element.38.refs_2_, bf16[2,200,1024]{2,1,0:T(8,128)(2,1)} %refs_2_.4), custom_call_target="tpu_custom_call" | custom-call | flops 13421772800 | tf_op jit(solution)/shard_map/up3/pallas_call | solution.py:236
  104.1 33.3 %down4.1 = (bf16[2048,1024]{1,0:T(8,128)(2,1)}, bf16[2,2,2,2,64,3200]{5,4,3,2,1,0:T(8,128)(2,1)}) custom-call(bf16[2048,3200]{1,0:T(8,128)(2,1)} %get-tuple-element.39.refs_0_, bf16[3200,1024]{1,0:T(8,128)(2,1)} %bitcast.21, bf16[2048,1024]{1,0:T(8,128)(2,1)} %bitcast.41, bf16[2,64,3200]{2,1,0:T(8,128)(2,1)} %refs_3_.3), custom_call_target="tpu_custom_call" | custom-call | flops 13421772800 | tf_op jit(solution)/shard_map/down4/pallas_call | solution.py:236
  137.5 36.1 %gate5.1 = (bf16[2048,1024]{1,0:T(8,128)(2,1)}, f32[2048,3200]{1,0:T(8,128)}, bf16[2,2,2,2,200,1024]{5,4,3,2,1,0:T(8,128)(2,1)}) custom-call(bf16[2048,1024]{1,0:T(8,128)(2,1)} %get-tuple-element.41.refs_0_.refs_4_, bf16[1024,3200]{1,0:T(8,128)(2,1)} %bitcast.45, bf16[2,200,1024]{2,1,0:T(8,128)(2,1)} %refs_2_.4), custom_call_target="tpu_custom_call" | custom-call | flops 13421772800 | tf_op jit(solution)/shard_map/gate5/pallas_call | solution.py:236
  173.5 33.4 %hidden_back6.1 = (bf16[2048,3200]{1,0:T(8,128)(2,1)}, bf16[2,2,2,2,64,3200]{5,4,3,2,1,0:T(8,128)(2,1)}) custom-call(bf16[2048,1024]{1,0:T(8,128)(2,1)} %bitcast.42, bf16[3200,1024]{1,0:T(8,128)(2,1)} %bitcast.51, bf16[2,64,3200]{2,1,0:T(8,128)(2,1)} %refs_2_.5), custom_call_target="tpu_custom_call" | custom-call | flops 13421772800 | tf_op jit(solution)/shard_map/hidden_back6/pallas_call | solution.py:236
  207.0 39.4 %up_back7.1 = (bf16[2048,3200]{1,0:T(8,128)(2,1)}, bf16[2048,3200]{1,0:T(8,128)(2,1)}, bf16[2048,3200]{1,0:T(8,128)(2,1)}) custom-call(bf16[2048,1024]{1,0:T(8,128)(2,1)} %get-tuple-element.43.refs_0_.refs_1_, bf16[1024,3200]{1,0:T(8,128)(2,1)} %bitcast.23, f32[2048,3200]{1,0:T(8,128)} %get-tuple-element.46.refs_2_, bf16[2048,3200]{1,0:T(8,128)(2,1)} %get-tuple-element.47.refs_3_), custom_call_target="tpu_custom_call" | custom-call | flops 13421772800 | tf_op jit(solution)/shard_map/up_back7/pallas_call | solution.py:236
  246.3 18.6 %weight_back8.1 = bf16[3200,1024]{1,0:T(8,128)(2,1)} custom-call(bf16[2048,3200]{1,0:T(8,128)(2,1)} %get-tuple-element.50.refs_0_, bf16[2048,1024]{1,0:T(8,128)(2,1)} %bitcast.43), custom_call_target="tpu_custom_call" | custom-call | flops 13421772800 | tf_op jit(solution)/shard_map/weight_back8/pallas_call | solution.py:236
  264.9 37.1 %weight_back9.1 = (bf16[1024,3200]{1,0:T(8,128)(2,1)}, bf16[200,1024]{1,0:T(8,128)(2,1)}) custom-call(bf16[2048,3200]{1,0:T(8,128)(2,1)} %get-tuple-element.48.refs_0_, bf16[2048,1024]{1,0:T(8,128)(2,1)} %get-tuple-element.43.refs_0_.refs_1_, bf16[2,2,2,2,200,1024]{5,4,3,2,1,0:T(8,128)(2,1)} %bitcast.52), custom_call_target="tpu_custom_call" | custom-call | flops 13421772800 | tf_op jit(solution)/shard_map/weight_back9/pallas_call | solution.py:236
  302.0 50.1 %state_back11.1 = (bf16[2048,1024]{1,0:T(8,128)(2,1)}, bf16[64,3200]{1,0:T(8,128)(2,1)}) custom-call(bf16[2048,3200]{1,0:T(8,128)(2,1)} %get-tuple-element.48.refs_0_, bf16[2048,3200]{1,0:T(8,128)(2,1)} %get-tuple-element.49.refs_1_.refs_0_, bf16[1024,3200]{1,0:T(8,128)(2,1)} %bitcast.46, bf16[1024,3200]{1,0:T(8,128)(2,1)} %bitcast.24, ...), custom_call_target="tpu_custom_call" | custom-call | flops 26843545600 | tf_op jit(solution)/shard_map/state_back11/pallas_call | solution.py:236
  352.2 19.1 %weight_back10.1 = bf16[1024,3200]{1,0:T(8,128)(2,1)} custom-call(bf16[2048,3200]{1,0:T(8,128)(2,1)} %get-tuple-element.49.refs_1_.refs_0_, bf16[2048,1024]{1,0:T(8,128)(2,1)} %get-tuple-element.43.refs_0_.refs_1_), custom_call_target="tpu_custom_call" | custom-call | flops 13421772800 | tf_op jit(solution)/shard_map/weight_back10/pallas_call | solution.py:236
  371.2 18.6 %weight_back13.1 = bf16[3200,1024]{1,0:T(8,128)(2,1)} custom-call(bf16[2048,3200]{1,0:T(8,128)(2,1)} %get-tuple-element.39.refs_0_, bf16[2048,1024]{1,0:T(8,128)(2,1)} %get-tuple-element.52.refs_0_.refs_1_), custom_call_target="tpu_custom_call" | custom-call | flops 13421772800 | tf_op jit(solution)/shard_map/weight_back13/pallas_call | solution.py:236
  389.8 44.1 %gated_back12.1 = (bf16[2048,3200]{1,0:T(8,128)(2,1)}, bf16[2048,3200]{1,0:T(8,128)(2,1)}, bf16[64,3200]{1,0:T(8,128)(2,1)}) custom-call(bf16[2048,1024]{1,0:T(8,128)(2,1)} %get-tuple-element.52.refs_0_.refs_1_, bf16[3200,1024]{1,0:T(8,128)(2,1)} %bitcast.22, f32[2048,3200]{1,0:T(8,128)} %get-tuple-element.38.refs_2_, ...), custom_call_target="tpu_custom_call" | custom-call | flops 13421772800 | tf_op jit(solution)/shard_map/gated_back12/pallas_call | solution.py:236
  434.0 36.6 %weight_back14.1 = (bf16[1024,3200]{1,0:T(8,128)(2,1)}, bf16[200,1024]{1,0:T(8,128)(2,1)}) custom-call(bf16[2048,3200]{1,0:T(8,128)(2,1)} %get-tuple-element.55.refs_0_, bf16[2048,1024]{1,0:T(8,128)(2,1)} %get-tuple-element.36.refs_0_.refs_1_, bf16[2,2,2,2,200,1024]{5,4,3,2,1,0:T(8,128)(2,1)} %bitcast.47), custom_call_target="tpu_custom_call" | custom-call | flops 13421772800 | tf_op jit(solution)/shard_map/weight_back14/pallas_call | solution.py:236
  470.6 2.0 fusion.11
  472.6 34.9 %weight_back15.1 = (bf16[1024,3200]{1,0:T(8,128)(2,1)}, bf16[64,3200]{1,0:T(8,128)(2,1)}) custom-call(bf16[2048,3200]{1,0:T(8,128)(2,1)} %get-tuple-element.54.refs_0_, bf16[2048,1024]{1,0:T(8,128)(2,1)} %get-tuple-element.36.refs_0_.refs_1_, bf16[2,2,2,2,64,3200]{5,4,3,2,1,0:T(8,128)(2,1)} %bitcast.49), custom_call_target="tpu_custom_call" | custom-call | flops 13421772800 | tf_op jit(solution)/shard_map/weight_back15/pallas_call | solution.py:236
  507.5 28.1 %add.103 = bf16[64,3200]{1,0:T(8,128)(2,1)} custom-call(bf16[2,2,2,2,64,3200]{5,4,3,2,1,0:T(8,128)(2,1)} %bitcast.26), custom_call_target="tpu_custom_call" | custom-call | tf_op jit(solution)/shard_map/add/pallas_call | solution.py:236
  535.7 0.0 copy-start.2
  535.7 2.5 fusion.9
  540.1 0.6 broadcast_in_dim.3.refs_0_
  540.7 10.3 %squares.1 = f32[8,128]{1,0:T(8,128)} custom-call(f32[8,128]{1,0:T(8,128)} %broadcast_in_dim.3.refs_0_), custom_call_target="tpu_custom_call" | custom-call | tf_op jit(solution)/shard_map/squares/pallas_call | solution.py:236
  551.0 1.2 slice.3
  552.9 0.0 copy-start.1
  553.0 0.0 copy-start.3
  553.0 0.0 copy-start.4
  553.0 4.7 fusion.17
  557.7 0.0 copy-start.11
  557.7 2.4 fusion.8
  560.2 1.0 copy-done.6
  561.2 0.1 copy-done.8
  561.3 0.3 copy-done.11
  561.6 2.4 fusion.14
  (16 shorter events, 0.0 us)
Async XLA Ops:
  434.0 36.6 %copy-start.10 = (bf16[200,1024]{1,0:T(8,128)(2,1)S(1)}, bf16[200,1024]{1,0:T(8,128)(2,1)}, u32[]{:S(2)}) copy-start(bf16[200,1024]{1,0:T(8,128)(2,1)} %get-tuple-element.62) | copy-start | bytes 1228804
  535.7 17.3 %copy-start.2 = (f32[2,200,1024]{2,1,0:T(8,128)S(1)}, f32[2,200,1024]{2,1,0:T(8,128)}, u32[]{:S(2)}) copy-start(f32[2,200,1024]{2,1,0:T(8,128)} %param.21) | copy-start | bytes 4915204
  552.9 4.7 copy-start.1
  553.0 4.7 copy-start.3
  553.0 4.7 copy-start.4
  553.0 4.7 copy-start.7
  553.0 4.7 copy-start.9
  557.7 2.5 copy-start
  557.7 2.5 copy-start.5
  557.7 3.5 copy-start.6
  557.7 3.6 copy-start.8
  557.7 3.8 copy-start.11
